TPU v7x, 32 devices: a whole 2x2x4 slice. The times are simulated.
32 devices in a mesh: grp: 2 (over y), pulse: 4 (over z), chan: 2 (over x), sub: 2 (over core).
Axes of the slice: x: 2, y: 2, z: 4, core: 2. Of those that a mesh axis runs over, the one named last changes fastest.
Arguments:
- samples: int32 [2, 16, 512, 4096], P(None, ('grp', 'chan', 'sub'), 'pulse'), parts along dimension 1, may hold values from -2048 to 2047
- replica: float32 [2, 4096], replicated, may hold values from -6 to 6
- window: int32 [16, 2], P(('grp', 'chan', 'sub')), parts along dimension 0, may hold values from 1 to 28, as said below
- thresh: int32 [16, 2], P(('grp', 'chan', 'sub')), parts along dimension 0, may hold values from 2 to 32, as said below
Outputs:
- ratio_map: float32 [16, 512, 4096], P(('grp', 'chan', 'sub'), None, 'pulse'), parts along dimension 0
- detections: float32 [2], P('grp'), parts along dimension 0
There are 2 independent parts, one for each index of `grp`. A program takes and returns all parts, laid end to end along the dimension named above; an argument that names none is the same for every part. Nothing has to cross between parts.
Inputs may be any that keep to these rules, and one draw needn't show every extreme that they name: `window`: column 0 is a channel's guard gates on each side, 1 to 4; column 1 its training gates on each side, 14 to 28; some channel has both at their most. `thresh`: column 0 is a numerator of 8 to 32, column 1 a denominator of 2 to 4.
All inputs are finite; a program needn't handle non-finite values.
Results may differ from a plain program's by a relative error of at most 0.0003.
Values sent between devices are 32-bit elements; how exact they have to be, the bound alone decides.
A program may use at most 128 MiB of HBM per device.

v0:
```python
import functools
import math

import jax
import jax.numpy as jnp
import numpy as np
from jax import lax
from jax.experimental import pallas as pl
from jax.experimental.pallas import tpu as pltpu
from jax.sharding import PartitionSpec as P

GUARD_MAX = 4
TRAIN_MAX = 28
MARGIN = GUARD_MAX + TRAIN_MAX
EPSILON = 1e-06
INPUT_SCALE = 1.0 / 2048.0
LANES = 128
SUB = 8
RADIX = 4


def halves(table):
    hi = np.asarray(table, np.float32).astype(jnp.bfloat16)
    lo = (np.asarray(table, np.float64) - hi.astype(np.float64)).astype(jnp.bfloat16)
    return hi, lo


def lane_table(sign):
    idx = np.arange(LANES)
    ang = 2.0 * np.pi * ((idx[:, None] * idx[None, :]) % LANES) / LANES
    c, s = np.cos(ang), sign * np.sin(ang)
    full = np.block([[c, s], [-s, c]])
    hi, lo = halves(full)
    return np.concatenate([hi, hi, lo], axis=0)


def doppler_table(pulses):
    part = pulses // RADIX
    m = np.arange(part)
    out = []
    for res in range(RADIX):
        ang = 2.0 * np.pi * ((m[None, :] * (RADIX * m[:, None] + res)) % pulses) / pulses
        c, s = np.cos(ang) / math.sqrt(pulses), -np.sin(ang) / math.sqrt(pulses)
        full = np.block([[c, -s], [s, c]])
        hi, lo = halves(full)
        out.append(np.concatenate([hi, hi, lo], axis=1))
    return np.stack(out)


def split(x, axis):
    hi = x.astype(jnp.bfloat16)
    lo = (x - hi.astype(jnp.float32)).astype(jnp.bfloat16)
    return jnp.concatenate([hi, lo, hi], axis=axis)


def fft_list(re, im, sign):
    n = len(re)
    if n == 1:
        return re, im
    er, ei = fft_list(re[0::2], im[0::2], sign)
    odd_r, odd_i = fft_list(re[1::2], im[1::2], sign)
    half = n // 2
    out_r, out_i = [None] * n, [None] * n
    for k in range(half):
        a, b = odd_r[k], odd_i[k]
        if k == 0:
            tr, ti = a, b
        elif 4 * k == n:
            tr, ti = (b, -a) if sign < 0 else (-b, a)
        elif 8 * k == n or 8 * k == 3 * n:
            h = math.sqrt(0.5)
            c = h if 8 * k == n else -h
            tr = c * a - (sign * h) * b
            ti = c * b + (sign * h) * a
        else:
            c = math.cos(2.0 * math.pi * k / n)
            s = sign * math.sin(2.0 * math.pi * k / n)
            tr = c * a - s * b
            ti = s * a + c * b
        out_r[k], out_i[k] = er[k] + tr, ei[k] + ti
        out_r[k + half], out_i[k + half] = er[k] - tr, ei[k] - ti
    return out_r, out_i


def range_kernel(n, rows, x_ref, tw1, rep, tw2, wf, wi, *rest):
    outs = rest[:n]
    cols = x_ref.shape[-1] // LANES
    per = cols // n

    def body(g, carry):
        r0 = pl.multiple_of(g * SUB, SUB)
        re = [x_ref[0, 0, pl.ds(r0, SUB), a * LANES:(a + 1) * LANES].astype(jnp.float32) for a in range(cols)]
        im = [x_ref[1, 0, pl.ds(r0, SUB), a * LANES:(a + 1) * LANES].astype(jnp.float32) for a in range(cols)]
        re, im = fft_list(re, im, -1.0)
        mr, mi = jnp.concatenate(re, axis=0), jnp.concatenate(im, axis=0)
        tr, ti = tw1[0], tw1[1]
        m = jnp.concatenate([mr * tr - mi * ti, mr * ti + mi * tr], axis=1)
        f = jnp.dot(split(m, 1), wf[...], preferred_element_type=jnp.float32)
        fr, fi = f[:, :LANES], f[:, LANES:]
        tr, ti = rep[0], rep[1]
        m = jnp.concatenate([fr * tr - fi * ti, fr * ti + fi * tr], axis=1)
        f = jnp.dot(split(m, 1), wi[...], preferred_element_type=jnp.float32)
        fr, fi = f[:, :LANES], f[:, LANES:]
        tr, ti = tw2[0], tw2[1]
        mr, mi = fr * tr - fi * ti, fr * ti + fi * tr
        re = [mr[a * SUB:(a + 1) * SUB] for a in range(cols)]
        im = [mi[a * SUB:(a + 1) * SUB] for a in range(cols)]
        re, im = fft_list(re, im, 1.0)
        for j in range(n):
            for a in range(per):
                outs[j][0, pl.ds(r0, SUB), a * LANES:(a + 1) * LANES] = re[j * per + a]
                outs[j][1, pl.ds(r0, SUB), a * LANES:(a + 1) * LANES] = im[j * per + a]
        return carry

    lax.fori_loop(0, rows // SUB, body, 0, unroll=2)


def range_compress(n, channel, samples, tw1, rep, tw2, wf, wi):
    _, _, pulses, gates = samples.shape
    rows = min(32, pulses)
    whole = lambda a: pl.BlockSpec(a.shape, lambda i: (0,) * a.ndim)
    return pl.pallas_call(
        functools.partial(range_kernel, n, rows),
        grid=(pulses // rows,),
        in_specs=[pl.BlockSpec((2, 1, rows, gates), lambda i: (0, channel, i, 0))]
        + [whole(a) for a in (tw1, rep, tw2, wf, wi)],
        out_specs=[pl.BlockSpec((2, rows, gates // n), lambda i: (0, i, 0))] * n,
        out_shape=[jax.ShapeDtypeStruct((2, pulses, gates // n), jnp.float32)] * n,
        compiler_params=pltpu.CompilerParams(vmem_limit_bytes=60 << 20),
        cost_estimate=pl.CostEstimate(flops=int(3e9), bytes_accessed=16 << 20, transcendentals=0),
    )(samples, tw1, rep, tw2, wf, wi)


def doppler_kernel(x0, x1, x2, x3, t_ref, p_ref):
    part = x0.shape[1]
    a, b, c, d = ([x[0], x[1]] for x in (x0, x1, x2, x3))
    sr, si = a[0] + c[0], a[1] + c[1]
    dr, di = a[0] - c[0], a[1] - c[1]
    ur, ui = b[0] + d[0], b[1] + d[1]
    vr, vi = b[0] - d[0], b[1] - d[1]
    ys = [(sr + ur, si + ui), (dr + vi, di - vr), (sr - ur, si - ui), (dr - vi, di + vr)]
    for res in range(RADIX):
        y = jnp.concatenate(ys[res], axis=0)
        out = jnp.dot(t_ref[res], split(y, 0), preferred_element_type=jnp.float32)
        re, im = out[:part], out[part:]
        p_ref[res] = re * re + im * im


def doppler_power(blocks, table):
    _, part, gates = blocks[0].shape
    width = min(256, gates)
    return pl.pallas_call(
        doppler_kernel,
        grid=(gates // width,),
        in_specs=[pl.BlockSpec((2, part, width), lambda i: (0, 0, i))] * RADIX
        + [pl.BlockSpec(table.shape, lambda i: (0, 0, 0))],
        out_specs=pl.BlockSpec((RADIX, part, width), lambda i: (0, 0, i)),
        out_shape=jax.ShapeDtypeStruct((RADIX, part, gates), jnp.float32),
        compiler_params=pltpu.CompilerParams(vmem_limit_bytes=40 << 20),
        cost_estimate=pl.CostEstimate(flops=int(3e9), bytes_accessed=8 << 20, transcendentals=0),
    )(*blocks, table)


def cfar_kernel(channel, scale_ref, p_ref, l_ref, r_ref, band_ref, cells_ref, *rest):
    out_ref, sum_ref, turn = rest[-3:]
    _, rows, gates = p_ref.shape
    width = band_ref.shape[-1]
    total = RADIX * rows
    core = p_ref[...].reshape(total, gates)
    zeros = jnp.zeros((total, LANES - MARGIN), jnp.float32)
    padded = jnp.concatenate(
        [zeros, l_ref[...].reshape(total, MARGIN), core, r_ref[...].reshape(total, MARGIN), zeros], axis=1
    )
    hi = padded.astype(jnp.bfloat16)
    lo = (padded - hi.astype(jnp.float32)).astype(jnp.bfloat16)
    band = band_ref[0]
    inv = scale_ref[channel, 1].astype(jnp.float32) / scale_ref[channel, 0].astype(jnp.float32)
    acc = jnp.zeros((SUB, LANES), jnp.float32)
    for g in range(gates // width):
        cut = slice(g * width, (g + 1) * width + 2 * LANES)
        noise = jnp.dot(hi[:, cut], band, preferred_element_type=jnp.float32) + jnp.dot(
            lo[:, cut], band, preferred_element_type=jnp.float32
        )
        here = slice(g * width, (g + 1) * width)
        ratio = core[:, here] * cells_ref[0, :, here] / (noise + EPSILON)
        for c in range(width // LANES):
            lanes = slice(c * LANES, (c + 1) * LANES)
            for res in range(RADIX):
                turn[g, c, pl.ds(res, rows, stride=RADIX), :] = ratio[res * rows:(res + 1) * rows, lanes]
            out_ref[0, :, g * width + c * LANES:g * width + (c + 1) * LANES] = turn[g, c]
        soft = jnp.clip(ratio * inv - 1.0, 0.0, 1.0)
        for c in range(width // LANES):
            acc = acc + jnp.sum(soft[:, c * LANES:(c + 1) * LANES].reshape(total // SUB, SUB, LANES), axis=0)

    @pl.when(pl.program_id(0) == 0)
    def _():
        sum_ref[...] = jnp.zeros_like(sum_ref)

    sum_ref[...] += acc


def cfar(channel, channels, power, left, right, band, cells, thresh, prior):
    _, part, gates = power.shape
    rows = min(32, part)
    width = band.shape[-1]
    specs = [
        pl.BlockSpec(memory_space=pltpu.SMEM),
        pl.BlockSpec((RADIX, rows, gates), lambda i: (0, i, 0)),
        pl.BlockSpec((RADIX, rows, MARGIN), lambda i: (0, i, 0)),
        pl.BlockSpec((RADIX, rows, MARGIN), lambda i: (0, i, 0)),
        pl.BlockSpec((1,) + band.shape[1:], lambda i: (channel, 0, 0)),
        pl.BlockSpec((1,) + cells.shape[1:], lambda i: (channel, 0, 0)),
    ]
    args = [thresh, power, left, right, band, cells]
    aliases = {}
    if prior is not None:
        specs.append(pl.BlockSpec(memory_space=pl.ANY))
        args.append(prior)
        aliases = {6: 0}
    return pl.pallas_call(
        functools.partial(cfar_kernel, channel),
        grid=(part // rows,),
        in_specs=specs,
        out_specs=[
            pl.BlockSpec((1, RADIX * rows, gates), lambda i: (channel, i, 0)),
            pl.BlockSpec((SUB, LANES), lambda i: (0, 0)),
        ],
        out_shape=[
            jax.ShapeDtypeStruct((channels, RADIX * part, gates), jnp.float32),
            jax.ShapeDtypeStruct((SUB, LANES), jnp.float32),
        ],
        input_output_aliases=aliases,
        scratch_shapes=[pltpu.VMEM((gates // width, width // LANES, RADIX * rows, LANES), jnp.float32)],
        compiler_params=pltpu.CompilerParams(vmem_limit_bytes=40 << 20),
        cost_estimate=pl.CostEstimate(flops=int(2e9), bytes_accessed=5 << 20, transcendentals=0),
    )(*args)


def sum_over(x, axis):
    size = lax.axis_size(axis)
    if size & (size - 1):
        return lax.psum(x, axis)
    bit = 1
    while bit < size:
        x = x + lax.ppermute(x, axis, [(i, i ^ bit) for i in range(size)])
        bit *= 2
    return x


def local(samples, replica, window, thresh):
    _, channels, part, gates = samples.shape
    n = lax.axis_size("pulse")
    me = lax.axis_index("pulse")
    cols = gates // LANES
    pulses = part * n
    own = gates // n

    k1 = np.arange(cols)[:, None]
    b = np.arange(LANES)[None, :]
    ang = 2.0 * np.pi * ((k1 * b) % gates) / gates
    tw1 = np.repeat(np.stack([np.cos(ang), -np.sin(ang)]), SUB, axis=1).astype(np.float32)
    turned = (jnp.asarray(k1 * b, jnp.int32) + own * me * jnp.asarray(k1, jnp.int32)) % gates
    ang2 = turned.astype(jnp.float32) * (2.0 * math.pi / gates)
    tw2 = jnp.repeat(jnp.stack([jnp.cos(ang2), jnp.sin(ang2)]), SUB, axis=1)
    rep = jnp.swapaxes(replica.reshape(2, LANES, cols), 1, 2) * (INPUT_SCALE / gates)
    rep = jnp.repeat(rep, SUB, axis=1)
    wf, wi = jnp.asarray(lane_table(-1.0)), jnp.asarray(lane_table(1.0))
    table = jnp.asarray(doppler_table(pulses))

    width = min(256, own)
    guard = window[:, 0][:, None, None]
    reach = guard + window[:, 1][:, None, None]
    dist = jnp.abs(
        jnp.arange(width + 2 * LANES, dtype=jnp.int32)[:, None] - LANES - jnp.arange(width, dtype=jnp.int32)[None, :]
    )[None]
    band = ((dist > guard) & (dist <= reach)).astype(jnp.bfloat16)
    gate = (me * own + jnp.arange(own, dtype=jnp.int32))[None, None, :]
    after = gates - 1 - gate
    cells = (
        jnp.minimum(gate, reach) - jnp.minimum(gate, guard) + jnp.minimum(after, reach) - jnp.minimum(after, guard)
    ).astype(jnp.float32)

    def shift(x, s):
        return lax.ppermute(x, "pulse", [(i, (i + s) % n) for i in range(n)])

    order = sorted(range(1, n), key=lambda s: -min(s, n - s))
    got = []
    for channel in range(channels):
        outs = range_compress(n, channel, samples, tw1, rep, tw2, wf, wi)
        blocks = [outs[0]] + [None] * (n - 1)
        for s in order:
            blocks[n - s] = shift(outs[s], s)
        got.append(blocks)

    ratio, sums = None, []
    up = [(i, i + 1) for i in range(n - 1)]
    down = [(i + 1, i) for i in range(n - 1)]
    for channel in range(channels):
        blocks = got[channel]
        if sums:
            blocks, sums = lax.optimization_barrier((blocks, sums))
        if n != RADIX:
            full = jnp.concatenate(blocks, axis=1)
            blocks = [full[:, q * (pulses // RADIX):(q + 1) * (pulses // RADIX)] for q in range(RADIX)]
        power = doppler_power(blocks, table)
        left = lax.ppermute(power[:, :, own - MARGIN:], "pulse", up)
        right = lax.ppermute(power[:, :, :MARGIN], "pulse", down)
        ratio, part_sum = cfar(channel, channels, power, left, right, band, cells, thresh, ratio)
        sums.append(part_sum)
    total = jnp.sum(functools.reduce(jnp.add, sums)) * (1024.0 / (pulses * gates))
    count = total.reshape(1)
    for axis in ("sub", "chan", "pulse"):
        count = sum_over(count, axis)
    return (ratio, count)


def solution(mesh):
    in_specs = (
        P(None, ("grp", "chan", "sub"), "pulse", None),
        P(),
        P(("grp", "chan", "sub"), None),
        P(("grp", "chan", "sub"), None),
    )
    out_specs = (P(("grp", "chan", "sub"), None, "pulse"), P("grp"))
    return jax.shard_map(local, mesh=mesh, in_specs=in_specs, out_specs=out_specs, check_vma=False)
```

profile of v0, /device:TPU:0, one launch (start us, length us, event | category | flops | bytes accessed | tf_op | source)
XLA Modules:
  0.0 245.7 jit_solution(13699785625243053718)
XLA Ops:
  0.6 0.8 broadcast_multiply_fusion
  2.3 0.9 cosine_bitcast_fusion
  3.1 0.8 broadcast_bitcast_fusion
  4.0 10.4 %shard_map.114 = (f32[2,128,1024]{2,1,0:T(8,128)}, f32[2,128,1024]{2,1,0:T(8,128)}, f32[2,128,1024]{2,1,0:T(8,128)}, f32[2,128,1024]{2,1,0:T(8,128)}) custom-call(s32[2,2,128,4096]{3,2,1,0:T(8,128)} %x_ref.3, f32[2,256,128]{2,1,0:T(8,128)} %constant.51.clone.tw1, f32[2,256,128]{2,1,0:T(8,128)} %get-tuple-element.47.rep, ...), custom_call_target="tpu_custom_call" | custom-call | flops 3000000000 | bytes 16777216 | tf_op jit(solution)/shard_map/pallas_call | solution.py:122
  14.4 5.1 %collective-permute-start.3 = (f32[2,128,1024]{2,1,0:T(8,128)}, f32[2,128,1024]{2,1,0:T(8,128)S(1)}, u32[]{:S(2)}, u32[]{:S(2)}) collective-permute-start(f32[2,128,1024]{2,1,0:T(8,128)} %get-tuple-element.24), channel_id=1, source_target_pairs={{0,12},{4,0},{8,4},{12,8},{1,13},{5,1},{9,5},{13,9},{2,14},{6,2},{... | collective-permute-start | bytes 3145736 | tf_op jit(solution)/shard_map/ppermute | solution.py:284
  19.5 1.0 collective-permute-start.5
  20.5 10.4 %shard_map.113 = (f32[2,128,1024]{2,1,0:T(8,128)}, f32[2,128,1024]{2,1,0:T(8,128)}, f32[2,128,1024]{2,1,0:T(8,128)}, f32[2,128,1024]{2,1,0:T(8,128)}) custom-call(s32[2,2,128,4096]{3,2,1,0:T(8,128)} %x_ref.3, f32[2,256,128]{2,1,0:T(8,128)} %constant.51.clone.tw1, f32[2,256,128]{2,1,0:T(8,128)} %get-tuple-element.47.rep, ...), custom_call_target="tpu_custom_call" | custom-call | flops 3000000000 | bytes 16777216 | tf_op jit(solution)/shard_map/pallas_call | solution.py:122
  30.9 2.8 %collective-permute-start = (f32[2,128,1024]{2,1,0:T(8,128)}, f32[2,128,1024]{2,1,0:T(8,128)S(1)}, u32[]{:S(2)}, u32[]{:S(2)}) collective-permute-start(f32[2,128,1024]{2,1,0:T(8,128)} %get-tuple-element.20), channel_id=1, source_target_pairs={{0,12},{4,0},{8,4},{12,8},{1,13},{5,1},{9,5},{13,9},{2,14},{6,2},{... | collective-permute-start | bytes 3145736 | tf_op jit(solution)/shard_map/ppermute | solution.py:284
  33.7 1.1 collective-permute-start.1
  35.4 7.9 %collective-permute-done.3.x1 = f32[2,128,1024]{2,1,0:T(8,128)S(1)} collective-permute-done((f32[2,128,1024]{2,1,0:T(8,128)}, f32[2,128,1024]{2,1,0:T(8,128)S(1)}, u32[]{:S(2)}, u32[]{:S(2)}) %collective-permute-start.3) | collective-permute-done | bytes 1048608 | tf_op jit(solution)/shard_map/ppermute | solution.py:284
  43.4 44.2 %collective-permute-start.2 = (f32[2,128,1024]{2,1,0:T(8,128)}, f32[2,128,1024]{2,1,0:T(8,128)S(1)}, u32[]{:S(2)}, u32[]{:S(2)}) collective-permute-start(f32[2,128,1024]{2,1,0:T(8,128)} %get-tuple-element.22), channel_id=1, source_target_pairs={{0,4},{4,8},{8,12},{12,0},{1,5},{5,9},{9,13},{13,1},{2,6},{6,10},{... | collective-permute-start | bytes 3145736 | tf_op jit(solution)/shard_map/ppermute | solution.py:284
  87.6 24.1 %collective-permute-done.4.x2 = f32[2,128,1024]{2,1,0:T(8,128)S(1)} collective-permute-done((f32[2,128,1024]{2,1,0:T(8,128)}, f32[2,128,1024]{2,1,0:T(8,128)S(1)}, u32[]{:S(2)}, u32[]{:S(2)}) %collective-permute-start.4) | collective-permute-done | bytes 1048608 | tf_op jit(solution)/shard_map/ppermute | solution.py:284
  111.7 1.4 copy-done.1
  113.1 1.2 copy-done.4
  114.3 3.3 %shard_map.115.p_ref = f32[4,128,1024]{2,1,0:T(8,128)S(1)} custom-call(f32[2,128,1024]{2,1,0:T(8,128)S(1)} %copy-done.4, f32[2,128,1024]{2,1,0:T(8,128)S(1)} %collective-permute-done.3.x1, f32[2,128,1024]{2,1,0:T(8,128)S(1)} %collective-permute-done.4.x2, f32[2,128,1024]{2,1,0:T(8,128)S(1)} %collective-permute-done.5.x3, bf16[4,256,768]{2,1,0:T(8,128)(2,1)S(1)} %copy-done.1), custom_call_target="tpu_custom_call" | custom-call | flops 3000000000 | bytes 8388608 | tf_op jit(solution)/shard_map/pallas_call | solution.py:152
  117.8 1.3 collective-permute-start.7
  119.1 47.1 %collective-permute-start.6 = (f32[4,128,32]{2,1,0:T(8,128)S(1)}, f32[4,128,32]{2,1,0:T(8,128)S(1)}, u32[]{:S(2)}, u32[]{:S(2)}) collective-permute-start(f32[4,128,32]{2,1,0:T(8,128)S(1)} %get-tuple-element.41), channel_id=1, source_target_pairs={{0,4},{4,8},{8,12},{1,5},{5,9},{9,13},{2,6},{6,10},{10,14},{3,7},{... | collective-permute-start | bytes 196616 | tf_op jit(solution)/shard_map/ppermute | solution.py:306
  166.3 2.9 %collective-permute-done.7.r_ref = f32[4,128,32]{2,1,0:T(8,128)S(1)} collective-permute-done((f32[4,128,32]{2,1,0:T(8,128)S(1)}, f32[4,128,32]{2,1,0:T(8,128)S(1)}, u32[]{:S(2)}, u32[]{:S(2)}) %collective-permute-start.7) | collective-permute-done | bytes 65568 | tf_op jit(solution)/shard_map/ppermute | solution.py:307
  169.1 1.2 collective-permute-done.6.l_ref
  170.3 3.8 %shard_map.116 = (f32[2,512,1024]{2,1,0:T(8,128)}, f32[8,128]{1,0:T(8,128)S(1)}) custom-call(s32[2,2]{1,0:T(2,128)S(1)} %copy-done, f32[4,128,1024]{2,1,0:T(8,128)S(1)} %shard_map.115.p_ref, f32[4,128,32]{2,1,0:T(8,128)S(1)} %collective-permute-done.6.l_ref, f32[4,128,32]{2,1,0:T(8,128)S(1)} %collective-permute-done.7.r_ref, ...), custom_call_target="tpu_custom_call" | custom-call | flops 2000000000 | bytes 5242880 | tf_op jit(solution)/shard_map/pallas_call | solution.py:220
  174.1 26.3 %collective-permute-done.1.x2 = f32[2,128,1024]{2,1,0:T(8,128)S(1)} collective-permute-done((f32[2,128,1024]{2,1,0:T(8,128)}, f32[2,128,1024]{2,1,0:T(8,128)S(1)}, u32[]{:S(2)}, u32[]{:S(2)}) %collective-permute-start.1) | collective-permute-done | bytes 1048608 | tf_op jit(solution)/shard_map/ppermute | solution.py:284
  200.4 3.3 %shard_map.117.p_ref = f32[4,128,1024]{2,1,0:T(8,128)S(1)} custom-call(f32[2,128,1024]{2,1,0:T(8,128)S(1)} %copy-done.3, f32[2,128,1024]{2,1,0:T(8,128)S(1)} %collective-permute-done.x1, f32[2,128,1024]{2,1,0:T(8,128)S(1)} %collective-permute-done.1.x2, f32[2,128,1024]{2,1,0:T(8,128)S(1)} %collective-permute-done.2.x3, bf16[4,256,768]{2,1,0:T(8,128)(2,1)S(1)} %copy-done.2), custom_call_target="tpu_custom_call" | custom-call | flops 3000000000 | bytes 8388608 | tf_op jit(solution)/shard_map/pallas_call | solution.py:152
  203.9 1.3 collective-permute-start.9
  205.2 11.8 %collective-permute-start.8 = (f32[4,128,32]{2,1,0:T(8,128)S(1)}, f32[4,128,32]{2,1,0:T(8,128)S(1)}, u32[]{:S(2)}, u32[]{:S(2)}) collective-permute-start(f32[4,128,32]{2,1,0:T(8,128)S(1)} %get-tuple-element.39), channel_id=1, source_target_pairs={{0,4},{4,8},{8,12},{1,5},{5,9},{9,13},{2,6},{6,10},{10,14},{3,7},{... | collective-permute-start | bytes 196616 | tf_op jit(solution)/shard_map/ppermute | solution.py:306
  217.0 3.8 %collective-permute-done.9.r_ref = f32[4,128,32]{2,1,0:T(8,128)S(1)} collective-permute-done((f32[4,128,32]{2,1,0:T(8,128)S(1)}, f32[4,128,32]{2,1,0:T(8,128)S(1)}, u32[]{:S(2)}, u32[]{:S(2)}) %collective-permute-start.9) | collective-permute-done | bytes 65568 | tf_op jit(solution)/shard_map/ppermute | solution.py:307
  220.9 1.2 collective-permute-done.8.l_ref
  222.0 3.8 %shard_map.118 = (f32[2,512,1024]{2,1,0:T(8,128)}, f32[8,128]{1,0:T(8,128)S(1)}) custom-call(s32[2,2]{1,0:T(2,128)S(1)} %copy-done, f32[4,128,1024]{2,1,0:T(8,128)S(1)} %shard_map.117.p_ref, f32[4,128,32]{2,1,0:T(8,128)S(1)} %collective-permute-done.8.l_ref, f32[4,128,32]{2,1,0:T(8,128)S(1)} %collective-permute-done.9.r_ref, ...), custom_call_target="tpu_custom_call", output_to_operand_aliasing={{0}: (6, {})} | custom-call | flops 2000000000 | bytes 5242880 | tf_op jit(solution)/shard_map/pallas_call | solution.py:220
  227.1 1.0 collective-permute-start.10
  229.1 2.8 %collective-permute-start.11 = (f32[1]{0:T(128)}, f32[1]{0:T(128)}, u32[]{:S(2)}, u32[]{:S(2)}) collective-permute-start(f32[1]{0:T(128)} %add.77), channel_id=1, source_target_pairs={{0,2},{2,0},{1,3},{3,1},{4,6},{6,4},{5,7},{7,5},{8,10},{10,8},{9,1... | collective-permute-start | bytes 20 | tf_op jit(solution)/shard_map/ppermute | solution.py:245
  231.9 0.9 collective-permute-done.11
  233.5 3.8 %collective-permute-start.12 = (f32[1]{0:T(128)}, f32[1]{0:T(128)}, u32[]{:S(2)}, u32[]{:S(2)}) collective-permute-start(f32[1]{0:T(128)} %add.78), channel_id=1, source_target_pairs={{0,4},{4,0},{8,12},{12,8},{1,5},{5,1},{9,13},{13,9},{2,6},{6,2},{1... | collective-permute-start | bytes 20 | tf_op jit(solution)/shard_map/ppermute | solution.py:245
  238.3 5.3 %collective-permute-start.13 = (f32[1]{0:T(128)}, f32[1]{0:T(128)}, u32[]{:S(2)}, u32[]{:S(2)}) collective-permute-start(f32[1]{0:T(128)} %add.79), channel_id=1, source_target_pairs={{0,8},{4,12},{8,0},{12,4},{1,9},{5,13},{9,1},{13,5},{2,10},{6,14},... | collective-permute-start | bytes 20 | tf_op jit(solution)/shard_map/ppermute | solution.py:245
  (31 shorter events, 3.5 us)
Async XLA Ops:
  14.4 29.0 %collective-permute-start.3 = (f32[2,128,1024]{2,1,0:T(8,128)}, f32[2,128,1024]{2,1,0:T(8,128)S(1)}, u32[]{:S(2)}, u32[]{:S(2)}) collective-permute-start(f32[2,128,1024]{2,1,0:T(8,128)} %get-tuple-element.24), channel_id=1, source_target_pairs={{0,12},{4,0},{8,4},{12,8},{1,13},{5,1},{9,5},{13,9},{2,14},{6,2},{... | collective-permute-start | bytes 3145736 | tf_op jit(solution)/shard_map/ppermute | solution.py:284
  19.5 92.2 %collective-permute-start.4 = (f32[2,128,1024]{2,1,0:T(8,128)}, f32[2,128,1024]{2,1,0:T(8,128)S(1)}, u32[]{:S(2)}, u32[]{:S(2)}) collective-permute-start(f32[2,128,1024]{2,1,0:T(8,128)} %get-tuple-element.25), channel_id=1, source_target_pairs={{0,8},{4,12},{8,0},{12,4},{1,9},{5,13},{9,1},{13,5},{2,10},{6,14},... | collective-permute-start | bytes 3145736 | tf_op jit(solution)/shard_map/ppermute | solution.py:284
  19.5 15.4 %copy-start.5 = (s32[2,2]{1,0:T(2,128)S(1)}, s32[2,2]{1,0:T(2,128)}, u32[]{:S(2)}) copy-start(s32[2,2]{1,0:T(2,128)} %param.12) | copy-start | bytes 52
  19.5 92.2 %collective-permute-start.5 = (f32[2,128,1024]{2,1,0:T(8,128)}, f32[2,128,1024]{2,1,0:T(8,128)S(1)}, u32[]{:S(2)}, u32[]{:S(2)}) collective-permute-start(f32[2,128,1024]{2,1,0:T(8,128)} %get-tuple-element.26), channel_id=1, source_target_pairs={{0,4},{4,8},{8,12},{12,0},{1,5},{5,9},{9,13},{13,1},{2,6},{6,10},{... | collective-permute-start | bytes 3145736 | tf_op jit(solution)/shard_map/ppermute | solution.py:284
  30.9 143.2 %collective-permute-start = (f32[2,128,1024]{2,1,0:T(8,128)}, f32[2,128,1024]{2,1,0:T(8,128)S(1)}, u32[]{:S(2)}, u32[]{:S(2)}) collective-permute-start(f32[2,128,1024]{2,1,0:T(8,128)} %get-tuple-element.20), channel_id=1, source_target_pairs={{0,12},{4,0},{8,4},{12,8},{1,13},{5,1},{9,5},{13,9},{2,14},{6,2},{... | collective-permute-start | bytes 3145736 | tf_op jit(solution)/shard_map/ppermute | solution.py:284
  33.7 166.7 %collective-permute-start.1 = (f32[2,128,1024]{2,1,0:T(8,128)}, f32[2,128,1024]{2,1,0:T(8,128)S(1)}, u32[]{:S(2)}, u32[]{:S(2)}) collective-permute-start(f32[2,128,1024]{2,1,0:T(8,128)} %get-tuple-element.21), channel_id=1, source_target_pairs={{0,8},{4,12},{8,0},{12,4},{1,9},{5,13},{9,1},{13,5},{2,10},{6,14},... | collective-permute-start | bytes 3145736 | tf_op jit(solution)/shard_map/ppermute | solution.py:284
  43.4 157.0 %collective-permute-start.2 = (f32[2,128,1024]{2,1,0:T(8,128)}, f32[2,128,1024]{2,1,0:T(8,128)S(1)}, u32[]{:S(2)}, u32[]{:S(2)}) collective-permute-start(f32[2,128,1024]{2,1,0:T(8,128)} %get-tuple-element.22), channel_id=1, source_target_pairs={{0,4},{4,8},{8,12},{12,0},{1,5},{5,9},{9,13},{13,1},{2,6},{6,10},{... | collective-permute-start | bytes 3145736 | tf_op jit(solution)/shard_map/ppermute | solution.py:284
  111.7 1.4 copy-start.1
  113.1 1.2 copy-start.4
  114.3 56.0 %copy-start = (s32[2,2]{1,0:T(2,128)S(1)}, s32[2,2]{1,0:T(2,128)}, u32[]{:S(2)}) copy-start(s32[2,2]{1,0:T(2,128)} %scale_ref.3) | copy-start | bytes 52
  117.8 51.4 %collective-permute-start.7 = (f32[4,128,32]{2,1,0:T(8,128)S(1)}, f32[4,128,32]{2,1,0:T(8,128)S(1)}, u32[]{:S(2)}, u32[]{:S(2)}) collective-permute-start(f32[4,128,32]{2,1,0:T(8,128)S(1)} %get-tuple-element.40), channel_id=1, source_target_pairs={{4,0},{8,4},{12,8},{5,1},{9,5},{13,9},{6,2},{10,6},{14,10},{7,3},{... | collective-permute-start | bytes 196616 | tf_op jit(solution)/shard_map/ppermute | solution.py:307
  119.1 51.2 %collective-permute-start.6 = (f32[4,128,32]{2,1,0:T(8,128)S(1)}, f32[4,128,32]{2,1,0:T(8,128)S(1)}, u32[]{:S(2)}, u32[]{:S(2)}) collective-permute-start(f32[4,128,32]{2,1,0:T(8,128)S(1)} %get-tuple-element.41), channel_id=1, source_target_pairs={{0,4},{4,8},{8,12},{1,5},{5,9},{9,13},{2,6},{6,10},{10,14},{3,7},{... | collective-permute-start | bytes 196616 | tf_op jit(solution)/shard_map/ppermute | solution.py:306
  166.3 34.2 %copy-start.2 = (bf16[4,256,768]{2,1,0:T(8,128)(2,1)S(1)}, bf16[4,256,768]{2,1,0:T(8,128)(2,1)}, u32[]{:S(2)}) copy-start(bf16[4,256,768]{2,1,0:T(8,128)(2,1)} %constant.50.clone.t_ref) | copy-start | bytes 4718596
  166.3 34.2 %copy-start.3 = (f32[2,128,1024]{2,1,0:T(8,128)S(1)}, f32[2,128,1024]{2,1,0:T(8,128)}, u32[]{:S(2)}) copy-start(f32[2,128,1024]{2,1,0:T(8,128)} %get-tuple-element.28.x0) | copy-start | bytes 3145732
  203.9 17.0 %collective-permute-start.9 = (f32[4,128,32]{2,1,0:T(8,128)S(1)}, f32[4,128,32]{2,1,0:T(8,128)S(1)}, u32[]{:S(2)}, u32[]{:S(2)}) collective-permute-start(f32[4,128,32]{2,1,0:T(8,128)S(1)} %get-tuple-element.38), channel_id=1, source_target_pairs={{4,0},{8,4},{12,8},{5,1},{9,5},{13,9},{6,2},{10,6},{14,10},{7,3},{... | collective-permute-start | bytes 196616 | tf_op jit(solution)/shard_map/ppermute | solution.py:307
  205.2 16.8 %collective-permute-start.8 = (f32[4,128,32]{2,1,0:T(8,128)S(1)}, f32[4,128,32]{2,1,0:T(8,128)S(1)}, u32[]{:S(2)}, u32[]{:S(2)}) collective-permute-start(f32[4,128,32]{2,1,0:T(8,128)S(1)} %get-tuple-element.39), channel_id=1, source_target_pairs={{0,4},{4,8},{8,12},{1,5},{5,9},{9,13},{2,6},{6,10},{10,14},{3,7},{... | collective-permute-start | bytes 196616 | tf_op jit(solution)/shard_map/ppermute | solution.py:306
  227.1 1.4 collective-permute-start.10
  229.1 3.7 %collective-permute-start.11 = (f32[1]{0:T(128)}, f32[1]{0:T(128)}, u32[]{:S(2)}, u32[]{:S(2)}) collective-permute-start(f32[1]{0:T(128)} %add.77), channel_id=1, source_target_pairs={{0,2},{2,0},{1,3},{3,1},{4,6},{6,4},{5,7},{7,5},{8,10},{10,8},{9,1... | collective-permute-start | bytes 20 | tf_op jit(solution)/shard_map/ppermute | solution.py:245
  233.5 4.2 %collective-permute-start.12 = (f32[1]{0:T(128)}, f32[1]{0:T(128)}, u32[]{:S(2)}, u32[]{:S(2)}) collective-permute-start(f32[1]{0:T(128)} %add.78), channel_id=1, source_target_pairs={{0,4},{4,0},{8,12},{12,8},{1,5},{5,1},{9,13},{13,9},{2,6},{6,2},{1... | collective-permute-start | bytes 20 | tf_op jit(solution)/shard_map/ppermute | solution.py:245
  238.3 5.6 %collective-permute-start.13 = (f32[1]{0:T(128)}, f32[1]{0:T(128)}, u32[]{:S(2)}, u32[]{:S(2)}) collective-permute-start(f32[1]{0:T(128)} %add.79), channel_id=1, source_target_pairs={{0,8},{4,12},{8,0},{12,4},{1,9},{5,13},{9,1},{13,5},{2,10},{6,14},... | collective-permute-start | bytes 20 | tf_op jit(solution)/shard_map/ppermute | solution.py:245
where the time goes:
time: 246 us
  starting transfers between devices  129 us (52%)
  waiting for transfers between devices  69.3 us (28%)
  Pallas kernels  35.1 us (14%)
  between operations  5.08 us (2%)
  local copies, waits for them, and re-layouts  4.13 us (2%)
  other arithmetic  3.39 us (1%)
    ppermute x2, starting transfers between devices, local(): left = lax.ppermute(power[:, :, own - MARGIN:], 'pulse', up)  58.9 us
    ppermute x6, waiting for transfers between devices, shift(): return lax.ppermute(x, 'pulse', [(i, (i + s) % n) for i in range(n)])  58.3 us
    ppermute x6, starting transfers between devices, shift(): return lax.ppermute(x, 'pulse', [(i, (i + s) % n) for i in range(n)])  54.2 us
    pallas_call x2, Pallas kernels, range_compress(): pl.pallas_call(functools.partial(range_kernel, n, rows), grid=(pulses //...  20.8 us
    ppermute x4, starting transfers between devices, sum_over(): x = x + lax.ppermute(x, axis, [(i, i ^ bit) for i in range(size)])  13 us
    pallas_call x2, Pallas kernels, cfar(): pl.pallas_call(functools.partial(cfar_kernel, channel), grid=(part // row...  7.61 us
    ppermute x2, waiting for transfers between devices, local(): right = lax.ppermute(power[:, :, :MARGIN], 'pulse', down)  6.67 us
    pallas_call x2, Pallas kernels, doppler_power(): pl.pallas_call(doppler_kernel, grid=(gates // width,), in_specs=[pl.Block...  6.62 us
  transfers between devices with their start and end apart: 14, of which 11 were waited for; matrix products, arithmetic and copies ran while one was open for 0% of the time, Pallas kernels for 7%

commit v1 on v0

v1 whole, which is shorter than its diff:
```python
import functools
import math

import jax
import jax.numpy as jnp
import numpy as np
from jax import lax
from jax.experimental import pallas as pl
from jax.experimental.pallas import tpu as pltpu
from jax.sharding import PartitionSpec as P

GUARD_MAX = 4
TRAIN_MAX = 28
MARGIN = GUARD_MAX + TRAIN_MAX
EPSILON = 1e-06
INPUT_SCALE = 1.0 / 2048.0
LANES = 128
SUB = 8
RADIX = 4


def halves(table):
    hi = np.asarray(table, np.float32).astype(jnp.bfloat16)
    lo = (np.asarray(table, np.float64) - hi.astype(np.float64)).astype(jnp.bfloat16)
    return hi, lo


MESH = pl.DeviceIdType.MESH
ROWS = 16
AHEAD = 3


def lane_table(sign):
    idx = np.arange(LANES)
    ang = 2.0 * np.pi * ((idx[:, None] * idx[None, :]) % LANES) / LANES
    c, s = np.cos(ang), sign * np.sin(ang)
    full = np.block([[c, s], [-s, c]])
    hi, lo = halves(full)
    return np.concatenate([hi, hi, lo], axis=0)


def doppler_table(pulses):
    part = pulses // RADIX
    m = np.arange(part)
    out = []
    for res in range(RADIX):
        ang = 2.0 * np.pi * ((m[None, :] * (RADIX * m[:, None] + res)) % pulses) / pulses
        c, s = np.cos(ang) / math.sqrt(pulses), -np.sin(ang) / math.sqrt(pulses)
        full = np.block([[c, -s], [s, c]])
        hi, lo = halves(full)
        out.append(np.concatenate([hi, hi, lo], axis=1))
    return np.stack(out)


def split(x, axis):
    hi = x.astype(jnp.bfloat16)
    lo = (x - hi.astype(jnp.float32)).astype(jnp.bfloat16)
    return jnp.concatenate([hi, lo, hi], axis=axis)


def fft_list(re, im, sign):
    n = len(re)
    if n == 1:
        return re, im
    er, ei = fft_list(re[0::2], im[0::2], sign)
    odd_r, odd_i = fft_list(re[1::2], im[1::2], sign)
    half = n // 2
    out_r, out_i = [None] * n, [None] * n
    for k in range(half):
        a, b = odd_r[k], odd_i[k]
        if k == 0:
            tr, ti = a, b
        elif 4 * k == n:
            tr, ti = (b, -a) if sign < 0 else (-b, a)
        elif 8 * k == n or 8 * k == 3 * n:
            h = math.sqrt(0.5)
            c = h if 8 * k == n else -h
            tr = c * a - (sign * h) * b
            ti = c * b + (sign * h) * a
        else:
            c = math.cos(2.0 * math.pi * k / n)
            s = sign * math.sin(2.0 * math.pi * k / n)
            tr = c * a - s * b
            ti = s * a + c * b
        out_r[k], out_i[k] = er[k] + tr, ei[k] + ti
        out_r[k + half], out_i[k + half] = er[k] - tr, ei[k] - ti
    return out_r, out_i


def range_rows(xs, c, r0, tw8, rep8, wf, wi, comp):
    n, per = comp.shape[1], comp.shape[2]
    cols = n * per
    rows = pl.ds(r0, SUB)
    re = [xs[0, c, rows, a * LANES:(a + 1) * LANES].astype(jnp.float32) for a in range(cols)]
    im = [xs[1, c, rows, a * LANES:(a + 1) * LANES].astype(jnp.float32) for a in range(cols)]
    re, im = fft_list(re, im, -1.0)
    mr, mi = jnp.concatenate(re, axis=0), jnp.concatenate(im, axis=0)
    tr, ti = tw8[0], tw8[1]
    m = jnp.concatenate([mr * tr - mi * ti, mr * ti + mi * tr], axis=1)
    f = jnp.dot(split(m, 1), wf[...], preferred_element_type=jnp.float32)
    fr, fi = f[:, :LANES], f[:, LANES:]
    tr, ti = rep8[0], rep8[1]
    m = jnp.concatenate([fr * tr - fi * ti, fr * ti + fi * tr], axis=1)
    f = jnp.dot(split(m, 1), wi[...], preferred_element_type=jnp.float32)
    fr, fi = f[:, :LANES], f[:, LANES:]
    tr, ti = tw8[0], tw8[1]
    mr, mi = fr * tr + fi * ti, fi * tr - fr * ti
    re = [mr[a * SUB:(a + 1) * SUB] for a in range(cols)]
    im = [mi[a * SUB:(a + 1) * SUB] for a in range(cols)]
    re, im = fft_list(re, im, 1.0)
    for j in range(n):
        for a in range(per):
            comp[c, j, a, 0, rows, :] = re[j * per + a]
            comp[c, j, a, 1, rows, :] = im[j * per + a]


def doppler_chunk(recv, c, g, table, pw, hi_ref, lo_ref):
    quarter = recv.shape[3] // RADIX
    a, b, cc, d = ([recv[c, g, ri, q * quarter:(q + 1) * quarter, :] for ri in range(2)] for q in range(RADIX))
    sr, si = a[0] + cc[0], a[1] + cc[1]
    dr, di = a[0] - cc[0], a[1] - cc[1]
    ur, ui = b[0] + d[0], b[1] + d[1]
    vr, vi = b[0] - d[0], b[1] - d[1]
    ys = [(sr + ur, si + ui), (dr + vi, di - vr), (sr - ur, si - ui), (dr - vi, di + vr)]
    for res in range(RADIX):
        y = jnp.concatenate(ys[res], axis=0)
        out = jnp.dot(table[res], split(y, 0), preferred_element_type=jnp.float32)
        re, im = out[:quarter], out[quarter:]
        p = re * re + im * im
        hi = p.astype(jnp.bfloat16)
        pw[c, g, res] = p
        hi_ref[c, g + 1, res] = hi
        lo_ref[c, g + 1, res] = (p - hi.astype(jnp.float32)).astype(jnp.bfloat16)


def cfar_chunk(c, g, first_gate, gates, thresh, window, pw, hi_ref, lo_ref, band, stage, acc):
    quarter = pw.shape[3]
    total = RADIX * quarter
    parts = [ref[c, g + k].reshape(total, LANES) for ref in (hi_ref, lo_ref) for k in range(3)]
    noise = jnp.dot(jnp.concatenate(parts, axis=1), band[c], preferred_element_type=jnp.float32)
    guard = window[c, 0]
    reach = guard + window[c, 1]
    gate = first_gate + g * LANES + lax.broadcasted_iota(jnp.int32, (SUB, LANES), 1)
    after = gates - 1 - gate
    cells = jnp.minimum(gate, reach) - jnp.minimum(gate, guard) + jnp.minimum(after, reach) - jnp.minimum(after, guard)
    cells = cells.astype(jnp.float32)[:1]
    inv = thresh[c, 1].astype(jnp.float32) / thresh[c, 0].astype(jnp.float32)
    ratio = pw[c, g].reshape(total, LANES) * cells / (noise + EPSILON)
    for res in range(RADIX):
        stage[c, g, pl.ds(res, quarter, stride=RADIX), :] = ratio[res * quarter:(res + 1) * quarter]
    soft = jnp.clip(ratio * inv - 1.0, 0.0, 1.0)
    acc[...] += jnp.sum(soft.reshape(total // SUB, SUB, LANES), axis=0)


def kernel(sizes, thresh, window, tw, rep, x_hbm, wf_hbm, wi_hbm, t_hbm, out_hbm, count,
           xs, wf, wi, table, tw8, rep8, comp, recv, pw, hi_ref, lo_ref, band, stage, pack, halo, gather, acc,
           in_sem, tab_sem, row_send, row_recv, chunk_send, chunk_recv, halo_send, halo_recv, out_sem, sum_sem):
    n, nx, ns, rows = sizes
    _, channels, part, gates = xs.shape
    chunks = comp.shape[2]
    quarter = pw.shape[3]
    pulses = RADIX * quarter
    own = gates // n
    blocks = part // rows
    last = channels - 1
    z, x, s = lax.axis_index("pulse"), lax.axis_index("chan"), lax.axis_index("sub")
    peers = n * nx * ns
    me = (z * nx + x) * ns + s
    h = n // 2
    half = z // h

    def peer(p):
        i = lax.rem(me + p, peers)
        return {"pulse": i // (nx * ns), "chan": lax.rem(i // ns, nx), "sub": lax.rem(i, ns)}

    barrier = pltpu.get_barrier_semaphore()

    def greet(p, carry):
        pl.semaphore_signal(barrier, 1, device_id=peer(p), device_id_type=MESH)
        return carry

    def load(b):
        c = b // blocks
        r = pl.ds(pl.multiple_of(lax.rem(b, blocks) * rows, rows), rows)
        return pltpu.make_async_copy(x_hbm.at[:, c, r, :], xs.at[:, c, r, :], in_sem.at[b])

    def start_load(b, carry):
        load(b).start()
        return carry

    tables = [pltpu.make_async_copy(a, b, tab_sem.at[i])
              for i, (a, b) in enumerate(((wf_hbm, wf), (wi_hbm, wi), (t_hbm, table)))]
    load(0).start()
    tables[0].start()
    tables[1].start()
    lax.fori_loop(1, channels * blocks, start_load, 0)
    tables[2].start()
    lax.fori_loop(1, peers, greet, 0)
    for k in range(tw.shape[1]):
        for ri in range(2):
            tw8[ri, k * SUB:(k + 1) * SUB, :] = jnp.broadcast_to(tw[ri, k:k + 1, :], (SUB, LANES))
            rep8[ri, k * SUB:(k + 1) * SUB, :] = jnp.broadcast_to(rep[ri, k:k + 1, :], (SUB, LANES))

    def near(k):
        return half * h + lax.rem(lax.rem(z, h) + 1 + k, h)

    def cross(k):
        return (1 - half) * h + lax.rem(z + s + k, h)

    def row_copy(c, dest, b):
        r = pl.multiple_of(b * rows, rows)
        return pltpu.make_async_remote_copy(
            comp.at[c, dest, :, :, pl.ds(r, rows), :],
            recv.at[c, :, :, pl.ds(pl.multiple_of(z * part + r, rows), rows), :],
            row_send.at[c, dest], row_recv.at[c, z],
            device_id={"pulse": dest}, device_id_type=MESH)

    def row_all(c, dest, src):
        return pltpu.make_async_remote_copy(
            comp.at[c, dest], recv.at[c, :, :, pl.ds(pl.multiple_of(src * part, part), part), :],
            row_send.at[c, dest], row_recv.at[c, src],
            device_id={"pulse": dest}, device_id_type=MESH)

    def chunk_copy(dest, src, g):
        return pltpu.make_async_remote_copy(
            comp.at[last, dest, g], recv.at[last, g, :, pl.ds(pl.multiple_of(src * part, part), part), :],
            chunk_send.at[dest, g], chunk_recv.at[src, g],
            device_id={"pulse": dest}, device_id_type=MESH)

    outer = jnp.logical_and(n == 4, jnp.logical_or(z == 0, z == n - 1))

    def row_near(c, b):
        for k in range(h - 1):
            row_copy(c, near(k), b).start()

    def row_cross(c, b):
        for k in range(h):
            row_copy(c, cross(k), b).start()

    def step(b, carry):
        c = b // blocks
        r0 = lax.rem(b, blocks) * rows
        load(b).wait()

        @pl.when(b == 0)
        def _():
            tables[0].wait()
            tables[1].wait()

        for u in range(rows // SUB):
            range_rows(xs, c, pl.multiple_of(r0 + u * SUB, SUB), tw8, rep8, wf, wi, comp)

        @pl.when(b == 1)
        def _():
            pl.semaphore_wait(barrier, peers - 1)

        @pl.when(jnp.logical_and(b >= 1, b <= last * blocks))
        def _():
            pc, pb = (b - 1) // blocks, lax.rem(b - 1, blocks)

            @pl.when(outer)
            def _():
                row_near(pc, pb)

            @pl.when(jnp.logical_not(outer))
            def _():
                row_cross(pc, pb)

        return carry

    lax.fori_loop(0, channels * blocks, step, 0)

    def each(body, lo, hi):
        def run(i, carry):
            body(i)
            return carry
        lax.fori_loop(lo, hi, run, 0)

    def order(k):
        odd = lax.rem(k, 2)
        return odd * (chunks - 1) + (1 - 2 * odd) * (k // 2)

    def rest(t):
        c, b = t // blocks, lax.rem(t, blocks)

        @pl.when(outer)
        def _():
            row_cross(c, b)

        @pl.when(jnp.logical_not(outer))
        def _():
            row_near(c, b)

    def last_near(k):
        for q in range(h - 1):
            chunk_copy(near(q), z, order(k)).start()

    def last_cross(k):
        for q in range(h):
            chunk_copy(cross(q), z, order(k)).start()

    ahead = min(AHEAD, chunks)
    each(last_near, 0, chunks)
    each(rest, 0, last * blocks)
    each(last_cross, 0, ahead)

    def keep(t):
        c, g = t // chunks, lax.rem(t, chunks)
        for ri in range(2):
            recv[c, g, ri, pl.ds(pl.multiple_of(z * part, part), part), :] = comp[c, z, g, ri]

    each(keep, 0, channels * chunks)
    q = lax.broadcasted_iota(jnp.int32, (3 * LANES, LANES), 0)
    j = lax.broadcasted_iota(jnp.int32, (3 * LANES, LANES), 1)
    dist = jnp.abs(q - LANES - j)
    for c in range(channels):
        guard = window[c, 0]
        reach = guard + window[c, 1]
        inside = jnp.where(dist > guard, 1.0, 0.0) * jnp.where(dist <= reach, 1.0, 0.0)
        inside = inside.astype(jnp.bfloat16)
        band[c] = jnp.concatenate([inside, inside], axis=0)
        blank = jnp.zeros((RADIX, quarter, LANES), jnp.bfloat16)
        for ref in (hi_ref, lo_ref):
            ref[c, 0] = blank
            ref[c, chunks + 1] = blank
    acc[...] = jnp.zeros_like(acc)
    tables[2].wait()

    def out_copy(c, g):
        lanes = pl.ds(pl.multiple_of(g * LANES, LANES), LANES)
        return pltpu.make_async_copy(stage.at[c, g], out_hbm.at[c, :, lanes], out_sem.at[c, g])

    def dop(c, g):
        doppler_chunk(recv, c, g, table, pw, hi_ref, lo_ref)

    def cfar(c, g):
        cfar_chunk(c, g, z * own, gates, thresh, window, pw, hi_ref, lo_ref, band, stage, acc)
        out_copy(c, g).start()

    def pack_left(c):
        pack[c, 0] = jnp.concatenate([pw[c, 0, res][:, :MARGIN] for res in range(RADIX)], axis=1)

    def pack_right(c):
        pack[c, 1] = jnp.concatenate([pw[c, chunks - 1, res][:, LANES - MARGIN:] for res in range(RADIX)], axis=1)

    def halo_copy(c, side, dest):
        return pltpu.make_async_remote_copy(
            pack.at[c, side], halo.at[c, 1 - side], halo_send.at[c, side], halo_recv.at[c, 1 - side],
            device_id={"pulse": dest}, device_id_type=MESH)

    def send_halo(c):
        @pl.when(z > 0)
        def _():
            halo_copy(c, 0, z - 1).start()

        @pl.when(z < n - 1)
        def _():
            halo_copy(c, 1, z + 1).start()

    def unpack(c, side):
        for res in range(RADIX):
            turn = (LANES - MARGIN - MARGIN * res if side == 0 else LANES - MARGIN * res) % LANES
            p = halo[c, side]
            if turn:
                p = pltpu.roll(p, turn, 1)
            hi = p.astype(jnp.bfloat16)
            at = 0 if side == 0 else chunks + 1
            hi_ref[c, at, res] = hi
            lo_ref[c, at, res] = (p - hi.astype(jnp.float32)).astype(jnp.bfloat16)

    def take_halo(c):
        @pl.when(z > 0)
        def _():
            halo_copy(c, 1, z).wait_recv()
            unpack(c, 0)

        @pl.when(z < n - 1)
        def _():
            halo_copy(c, 0, z).wait_recv()
            unpack(c, 1)

    for c in range(last):
        for o in range(1, n):
            row_all(c, z, lax.rem(z + o, n)).wait_recv()
        each(functools.partial(dop, c), 0, chunks)
        pack_left(c)
        pack_right(c)
        if chunks > 2:
            cfar(c, 1)
        send_halo(c)
        each(functools.partial(cfar, c), 2, chunks - 1)

    def arrive(k):
        for o in range(1, n):
            chunk_copy(z, lax.rem(z + o, n), order(k)).wait_recv()

    head = chunks - 1 if chunks >= 4 else chunks

    def last_step(k):
        @pl.when(k + ahead < chunks)
        def _():
            last_cross(k + ahead)

        arrive(k)
        dop(last, order(k))

        @pl.when(k == 0)
        def _():
            pack_left(last)

        @pl.when(k == min(1, chunks - 1))
        def _():
            pack_right(last)

        if chunks >= 4:
            @pl.when(k == 2)
            def _():
                send_halo(last)

            @pl.when(k >= 4)
            def _():
                cfar(last, order(k - 2))

    each(last_step, 0, head)
    if chunks < 4:
        send_halo(last)
        each(functools.partial(cfar, last), 1, chunks - 1)
    for c in range(channels):
        take_halo(c)
    edges = min(2, chunks)

    def edge(t):
        cfar(t // edges, lax.rem(t, edges) * (chunks - 1))

    each(edge, 0, channels * edges)
    if chunks >= 4:
        arrive(chunks - 1)
        dop(last, order(jnp.int32(chunks - 1)))
        each(lambda k: cfar(last, order(k)), chunks - 3, chunks)

    gather[me] = acc[...]
    for c in range(last):
        for o in range(1, n):
            row_all(c, lax.rem(z + o, n), z).wait_send()

    def sent(g):
        for o in range(1, n):
            chunk_copy(lax.rem(z + o, n), z, g).wait_send()

    each(sent, 0, chunks)
    for c in range(channels):
        @pl.when(z > 0)
        def _():
            halo_copy(c, 0, z - 1).wait_send()

        @pl.when(z < n - 1)
        def _():
            halo_copy(c, 1, z + 1).wait_send()

    def tell(p):
        pltpu.make_async_remote_copy(
            gather.at[me], gather.at[me], sum_sem.at[0], sum_sem.at[1],
            device_id=peer(p), device_id_type=MESH).start()

    each(tell, 1, peers)
    each(lambda t: out_copy(t // chunks, lax.rem(t, chunks)).wait(), 0, channels * chunks)
    every = pltpu.make_async_remote_copy(
        gather.at[pl.ds(0, peers - 1)], gather.at[pl.ds(0, peers - 1)], sum_sem.at[0], sum_sem.at[1],
        device_id=peer(1), device_id_type=MESH)
    every.wait()
    total = jnp.sum(gather[...], axis=0)
    count[0] = jnp.sum(total) * (1024.0 / (pulses * gates))


def local(samples, replica, window, thresh):
    _, channels, part, gates = samples.shape
    n, nx, ns = (lax.axis_size(a) for a in ("pulse", "chan", "sub"))
    cols = gates // LANES
    pulses = part * n
    own = gates // n
    chunks = own // LANES
    quarter = pulses // RADIX
    rows = min(ROWS, part)
    k1 = np.arange(cols)[:, None]
    b = np.arange(LANES)[None, :]
    ang = 2.0 * np.pi * ((k1 * b) % gates) / gates
    tw = np.stack([np.cos(ang), -np.sin(ang)]).astype(np.float32)
    rep = jnp.swapaxes(replica.reshape(2, LANES, cols), 1, 2) * (INPUT_SCALE / gates)
    wf, wi = lane_table(-1.0), lane_table(1.0)
    table = doppler_table(pulses)
    peers = n * nx * ns
    f32, bf16 = jnp.float32, jnp.bfloat16
    smem, vmem, hbm = (pl.BlockSpec(memory_space=m) for m in (pltpu.SMEM, pltpu.VMEM, pl.ANY))
    dma = pltpu.SemaphoreType.DMA
    return pl.pallas_call(
        functools.partial(kernel, (n, nx, ns, rows)),
        in_specs=[smem, smem, vmem, vmem, hbm, hbm, hbm, hbm],
        out_specs=[hbm, smem],
        out_shape=[jax.ShapeDtypeStruct((channels, pulses, own), f32), jax.ShapeDtypeStruct((1,), f32)],
        scratch_shapes=[
            pltpu.VMEM((2, channels, part, gates), jnp.int32),
            pltpu.VMEM(wf.shape, bf16),
            pltpu.VMEM(wi.shape, bf16),
            pltpu.VMEM(table.shape, bf16),
            pltpu.VMEM((2, cols * SUB, LANES), f32),
            pltpu.VMEM((2, cols * SUB, LANES), f32),
            pltpu.VMEM((channels, n, chunks, 2, part, LANES), f32),
            pltpu.VMEM((channels, chunks, 2, pulses, LANES), f32),
            pltpu.VMEM((channels, chunks, RADIX, quarter, LANES), f32),
            pltpu.VMEM((channels, chunks + 2, RADIX, quarter, LANES), bf16),
            pltpu.VMEM((channels, chunks + 2, RADIX, quarter, LANES), bf16),
            pltpu.VMEM((channels, 6 * LANES, LANES), bf16),
            pltpu.VMEM((channels, chunks, pulses, LANES), f32),
            pltpu.VMEM((channels, 2, quarter, LANES), f32),
            pltpu.VMEM((channels, 2, quarter, LANES), f32),
            pltpu.VMEM((peers, SUB, LANES), f32),
            pltpu.VMEM((SUB, LANES), f32),
            dma((channels * (part // rows),)),
            dma((3,)),
            dma((channels, n)),
            dma((channels, n)),
            dma((n, chunks)),
            dma((n, chunks)),
            dma((channels, 2)),
            dma((channels, 2)),
            dma((channels, chunks)),
            dma((2,)),
        ],
        compiler_params=pltpu.CompilerParams(
            collective_id=0, has_side_effects=True, vmem_limit_bytes=60 << 20),
        cost_estimate=pl.CostEstimate(flops=int(2e10), bytes_accessed=32 << 20, transcendentals=0),
    )(thresh, window, jnp.asarray(tw), rep, samples, jnp.asarray(wf), jnp.asarray(wi), jnp.asarray(table))


def solution(mesh):
    in_specs = (
        P(None, ("grp", "chan", "sub"), "pulse", None),
        P(),
        P(("grp", "chan", "sub"), None),
        P(("grp", "chan", "sub"), None),
    )
    out_specs = (P(("grp", "chan", "sub"), None, "pulse"), P("grp"))
    return jax.shard_map(lambda *a: tuple(local(*a)), mesh=mesh, in_specs=in_specs, out_specs=out_specs, check_vma=False)
```

time: 246 us -> 208 us (0.85)
  Pallas kernels: 35.1 us -> 199 us
  starting transfers between devices: 129 us -> 0 us
  waiting for transfers between devices: 69.3 us -> 0 us
  between operations: 5.08 us -> 2.39 us
  other arithmetic: 3.39 us -> 0.77 us
    pallas_call x6 -> x1, Pallas kernels: 35.1 us -> 199 us  [local(): pl.pallas_call(functools.partial(kernel, (n, nx, ns, rows)), in_specs=[sm...]
    ppermute x14 -> x0, starting transfers between devices: 129 us -> none  [the longest x2 58.9 us: local(): left = lax.ppermute(power[:, :, own - MARGIN:], 'pulse', up)]
    ppermute x14 -> x0, waiting for transfers between devices: 69.3 us -> none  [the longest x6 58.3 us: shift(): return lax.ppermute(x, 'pulse', [(i, (i + s) % n) for i in range(n)])]
  transfers between devices with their start and end apart: 14 -> 0, of which waited for: 11 -> 0; matrix products, arithmetic and copies ran while one was open for 0% -> 0% of each run, Pallas kernels for 7% -> 0%
where the time goes in v1:
time: 208 us
  Pallas kernels  199 us (96%)
  local copies, waits for them, and re-layouts  5.59 us (3%)
  between operations  2.39 us (1%)
    pallas_call x1, Pallas kernels, local(): pl.pallas_call(functools.partial(kernel, (n, nx, ns, rows)), in_specs=[sm...  199 us
    unnamed x1, local copies, waits for them, and re-layouts  4.79 us

profile of v1, /device:TPU:0, one launch (start us, length us, event | category | flops | bytes accessed | tf_op | source)
XLA Modules:
  0.0 207.9 jit_solution(13283896514718024681)
XLA Ops:
  0.6 0.8 broadcast_multiply_fusion
  1.4 0.1 mul.12
  1.5 0.7 copy.10
  2.2 199.2 %shard_map.95 = (f32[2,512,1024]{2,1,0:T(8,128)}, f32[1]{0:T(128)}) custom-call(s32[2,2]{1,0:T(2,128)} %thresh.1, s32[2,2]{1,0:T(2,128)} %window.1, f32[2,32,128]{2,1,0:T(8,128)} %constant.10.clone.tw, f32[2,32,128]{2,1,0:T(8,128)} %bitcast.1, s32[2,2,128,4096]{3,2,1,0:T(8,128)} %x_hbm.1, bf16[768,256]{1,0:T(8,128)(2,1)} %constant.11.clone.wf_hbm, ...), custom_call_target="tpu_custom_call" | custom-call | flops 20000000000 | bytes 33554432 | tf_op jit(solution)/shard_map/pallas_call | solution.py:495
  201.4 4.8 %copy.13 = f32[2,512,1024]{2,1,0:T(8,128)} copy(f32[2,512,1024]{2,1,0:T(8,128)} %get-tuple-element.4) | data formatting | bytes 8388608

commit v2 on v1

--- a/solution.py
+++ b/solution.py
@@ -133,7 +133,7 @@
         lo_ref[c, g + 1, res] = (p - hi.astype(jnp.float32)).astype(jnp.bfloat16)
 
 
-def cfar_chunk(c, g, first_gate, gates, thresh, window, pw, hi_ref, lo_ref, band, stage, acc):
+def cfar_chunk(c, g, first_gate, gates, thresh, window, pw, hi_ref, lo_ref, band, stage, out, acc):
     quarter = pw.shape[3]
     total = RADIX * quarter
     parts = [ref[c, g + k].reshape(total, LANES) for ref in (hi_ref, lo_ref) for k in range(3)]
@@ -147,14 +147,15 @@
     inv = thresh[c, 1].astype(jnp.float32) / thresh[c, 0].astype(jnp.float32)
     ratio = pw[c, g].reshape(total, LANES) * cells / (noise + EPSILON)
     for res in range(RADIX):
-        stage[c, g, pl.ds(res, quarter, stride=RADIX), :] = ratio[res * quarter:(res + 1) * quarter]
+        stage[pl.ds(res, quarter, stride=RADIX), :] = ratio[res * quarter:(res + 1) * quarter]
+    out[c, :, pl.ds(pl.multiple_of(g * LANES, LANES), LANES)] = stage[...]
     soft = jnp.clip(ratio * inv - 1.0, 0.0, 1.0)
     acc[...] += jnp.sum(soft.reshape(total // SUB, SUB, LANES), axis=0)
 
 
-def kernel(sizes, thresh, window, tw, rep, x_hbm, wf_hbm, wi_hbm, t_hbm, out_hbm, count,
-           xs, wf, wi, table, tw8, rep8, comp, recv, pw, hi_ref, lo_ref, band, stage, pack, halo, gather, acc,
-           in_sem, tab_sem, row_send, row_recv, chunk_send, chunk_recv, halo_send, halo_recv, out_sem, sum_sem):
+def kernel(sizes, rep_hbm, thresh_hbm, window_hbm, x_hbm, tw_hbm, wf_hbm, wi_hbm, t_hbm, out, count,
+           rep, thresh, window, tw, nat, xs, wf, wi, table, tw8, rep8, comp, recv, pw, hi_ref, lo_ref, band, stage, pack, halo, gather, acc,
+           in_sem, tab_sem, row_send, row_recv, chunk_send, chunk_recv, halo_send, halo_recv, sum_sem):
     n, nx, ns, rows = sizes
     _, channels, part, gates = xs.shape
     chunks = comp.shape[2]
@@ -189,17 +190,39 @@
         return carry
 
     tables = [pltpu.make_async_copy(a, b, tab_sem.at[i])
-              for i, (a, b) in enumerate(((wf_hbm, wf), (wi_hbm, wi), (t_hbm, table)))]
+              for i, (a, b) in enumerate(((rep_hbm, rep), (tw_hbm, tw), (wf_hbm, wf), (wi_hbm, wi), (t_hbm, table),
+                                         (thresh_hbm, thresh), (window_hbm, window)))]
+    tables[0].start()
     load(0).start()
-    tables[0].start()
-    tables[1].start()
+    for copy in tables[1:4]:
+        copy.start()
+    lax.fori_loop(1, peers, greet, 0)
     lax.fori_loop(1, channels * blocks, start_load, 0)
-    tables[2].start()
-    lax.fori_loop(1, peers, greet, 0)
-    for k in range(tw.shape[1]):
+    for copy in tables[4:]:
+        copy.start()
+    cols = tw.shape[1]
+    nat[...] = jnp.zeros_like(nat)
+    tables[0].wait()
+    for ri in range(2):
+        for k in range(cols):
+            nat[ri * cols + k:ri * cols + k + 1, :] = rep[ri:ri + 1, k * LANES:(k + 1) * LANES]
+    turned = jnp.transpose(nat[...])
+    row = lax.broadcasted_iota(jnp.int32, (LANES, LANES), 0)
+    lane = lax.broadcasted_iota(jnp.int32, (LANES, LANES), 1)
+    per = LANES // cols
+    for ri in range(2):
+        filt = jnp.zeros((cols, LANES), jnp.float32)
+        for k in range(per):
+            pick = jnp.where(jnp.logical_and(row >= ri * cols, lane == per * (row - ri * cols) + k), 1.0, 0.0)
+            filt = filt + jnp.dot(turned[k * cols:(k + 1) * cols], pick, precision=lax.Precision.HIGHEST,
+                                  preferred_element_type=jnp.float32)
+        filt = filt * (INPUT_SCALE / gates)
+        for k in range(cols):
+            rep8[ri, k * SUB:(k + 1) * SUB, :] = jnp.broadcast_to(filt[k:k + 1, :], (SUB, LANES))
+    tables[1].wait()
+    for k in range(cols):
         for ri in range(2):
             tw8[ri, k * SUB:(k + 1) * SUB, :] = jnp.broadcast_to(tw[ri, k:k + 1, :], (SUB, LANES))
-            rep8[ri, k * SUB:(k + 1) * SUB, :] = jnp.broadcast_to(rep[ri, k:k + 1, :], (SUB, LANES))
 
     def near(k):
         return half * h + lax.rem(lax.rem(z, h) + 1 + k, h)
@@ -244,8 +267,8 @@
 
         @pl.when(b == 0)
         def _():
-            tables[0].wait()
-            tables[1].wait()
+            tables[2].wait()
+            tables[3].wait()
 
         for u in range(rows // SUB):
             range_rows(xs, c, pl.multiple_of(r0 + u * SUB, SUB), tw8, rep8, wf, wi, comp)
@@ -295,9 +318,13 @@
         for q in range(h - 1):
             chunk_copy(near(q), z, order(k)).start()
 
+    def far(q):
+        return (1 - half) * (n - 1 - q) + half * q
+
     def last_cross(k):
+        end = k // (chunks - 1) if chunks > 1 else 1
         for q in range(h):
-            chunk_copy(cross(q), z, order(k)).start()
+            chunk_copy(end * far(q) + (1 - end) * cross(q), z, order(k)).start()
 
     ahead = min(AHEAD, chunks)
     each(last_near, 0, chunks)
@@ -310,6 +337,8 @@
             recv[c, g, ri, pl.ds(pl.multiple_of(z * part, part), part), :] = comp[c, z, g, ri]
 
     each(keep, 0, channels * chunks)
+    for copy in tables[4:]:
+        copy.wait()
     q = lax.broadcasted_iota(jnp.int32, (3 * LANES, LANES), 0)
     j = lax.broadcasted_iota(jnp.int32, (3 * LANES, LANES), 1)
     dist = jnp.abs(q - LANES - j)
@@ -324,18 +353,12 @@
             ref[c, 0] = blank
             ref[c, chunks + 1] = blank
     acc[...] = jnp.zeros_like(acc)
-    tables[2].wait()
-
-    def out_copy(c, g):
-        lanes = pl.ds(pl.multiple_of(g * LANES, LANES), LANES)
-        return pltpu.make_async_copy(stage.at[c, g], out_hbm.at[c, :, lanes], out_sem.at[c, g])
 
     def dop(c, g):
         doppler_chunk(recv, c, g, table, pw, hi_ref, lo_ref)
 
     def cfar(c, g):
-        cfar_chunk(c, g, z * own, gates, thresh, window, pw, hi_ref, lo_ref, band, stage, acc)
-        out_copy(c, g).start()
+        cfar_chunk(c, g, z * own, gates, thresh, window, pw, hi_ref, lo_ref, band, stage, out, acc)
 
     def pack_left(c):
         pack[c, 0] = jnp.concatenate([pw[c, 0, res][:, :MARGIN] for res in range(RADIX)], axis=1)
@@ -438,7 +461,7 @@
         dop(last, order(jnp.int32(chunks - 1)))
         each(lambda k: cfar(last, order(k)), chunks - 3, chunks)
 
-    gather[me] = acc[...]
+    gather[me] = jnp.sum(acc[...], axis=0, keepdims=True)
     for c in range(last):
         for o in range(1, n):
             row_all(c, lax.rem(z + o, n), z).wait_send()
@@ -463,7 +486,6 @@
             device_id=peer(p), device_id_type=MESH).start()
 
     each(tell, 1, peers)
-    each(lambda t: out_copy(t // chunks, lax.rem(t, chunks)).wait(), 0, channels * chunks)
     every = pltpu.make_async_remote_copy(
         gather.at[pl.ds(0, peers - 1)], gather.at[pl.ds(0, peers - 1)], sum_sem.at[0], sum_sem.at[1],
         device_id=peer(1), device_id_type=MESH)
@@ -485,19 +507,23 @@
     b = np.arange(LANES)[None, :]
     ang = 2.0 * np.pi * ((k1 * b) % gates) / gates
     tw = np.stack([np.cos(ang), -np.sin(ang)]).astype(np.float32)
-    rep = jnp.swapaxes(replica.reshape(2, LANES, cols), 1, 2) * (INPUT_SCALE / gates)
     wf, wi = lane_table(-1.0), lane_table(1.0)
     table = doppler_table(pulses)
     peers = n * nx * ns
     f32, bf16 = jnp.float32, jnp.bfloat16
-    smem, vmem, hbm = (pl.BlockSpec(memory_space=m) for m in (pltpu.SMEM, pltpu.VMEM, pl.ANY))
+    smem, vmem, hbm = (pl.BlockSpec(memory_space=m) for m in (pltpu.SMEM, pltpu.VMEM, pltpu.HBM))
     dma = pltpu.SemaphoreType.DMA
     return pl.pallas_call(
         functools.partial(kernel, (n, nx, ns, rows)),
-        in_specs=[smem, smem, vmem, vmem, hbm, hbm, hbm, hbm],
-        out_specs=[hbm, smem],
-        out_shape=[jax.ShapeDtypeStruct((channels, pulses, own), f32), jax.ShapeDtypeStruct((1,), f32)],
+        in_specs=[hbm] * 8,
+        out_specs=[vmem, smem],
+        out_shape=[pltpu.VMEM((channels, pulses, own), f32), jax.ShapeDtypeStruct((1,), f32)],
         scratch_shapes=[
+            pltpu.VMEM(replica.shape, f32),
+            pltpu.SMEM(thresh.shape, jnp.int32),
+            pltpu.SMEM(window.shape, jnp.int32),
+            pltpu.VMEM(tw.shape, f32),
+            pltpu.VMEM((LANES, LANES), f32),
             pltpu.VMEM((2, channels, part, gates), jnp.int32),
             pltpu.VMEM(wf.shape, bf16),
             pltpu.VMEM(wi.shape, bf16),
@@ -510,26 +536,26 @@
             pltpu.VMEM((channels, chunks + 2, RADIX, quarter, LANES), bf16),
             pltpu.VMEM((channels, chunks + 2, RADIX, quarter, LANES), bf16),
             pltpu.VMEM((channels, 6 * LANES, LANES), bf16),
-            pltpu.VMEM((channels, chunks, pulses, LANES), f32),
+            pltpu.VMEM((pulses, LANES), f32),
             pltpu.VMEM((channels, 2, quarter, LANES), f32),
             pltpu.VMEM((channels, 2, quarter, LANES), f32),
-            pltpu.VMEM((peers, SUB, LANES), f32),
+            pltpu.VMEM((peers, 1, LANES), f32),
             pltpu.VMEM((SUB, LANES), f32),
             dma((channels * (part // rows),)),
-            dma((3,)),
+            dma((7,)),
             dma((channels, n)),
             dma((channels, n)),
             dma((n, chunks)),
             dma((n, chunks)),
             dma((channels, 2)),
             dma((channels, 2)),
-            dma((channels, chunks)),
             dma((2,)),
         ],
         compiler_params=pltpu.CompilerParams(
-            collective_id=0, has_side_effects=True, vmem_limit_bytes=60 << 20),
+            collective_id=0, has_side_effects=True, vmem_limit_bytes=48 << 20),
         cost_estimate=pl.CostEstimate(flops=int(2e10), bytes_accessed=32 << 20, transcendentals=0),
-    )(thresh, window, jnp.asarray(tw), rep, samples, jnp.asarray(wf), jnp.asarray(wi), jnp.asarray(table))
+    )(*(pltpu.with_memory_space_constraint(jnp.asarray(a), pltpu.HBM)
+        for a in (replica, thresh, window, samples, tw, wf, wi, table)))
 
 
 def solution(mesh):

time: 208 us -> 203 us (0.976)
  local copies, waits for them, and re-layouts: 5.59 us -> 2.02 us
    unnamed x1, local copies, waits for them, and re-layouts: 4.79 us -> 2.02 us
where the time goes in v2:
time: 203 us
  Pallas kernels  198 us (98%)
  between operations  2.33 us (1%)
    pallas_call x1, Pallas kernels, local(): pl.pallas_call(functools.partial(kernel, (n, nx, ns, rows)), in_specs=[hb...  198 us

profile of v2, /device:TPU:0, one launch (start us, length us, event | category | flops | bytes accessed | tf_op | source)
XLA Modules:
  0.0 202.6 jit_solution(5561337616483513578)
XLA Ops:
  0.6 198.3 %shard_map.95 = (f32[2,512,1024]{2,1,0:T(8,128)S(1)}, f32[1]{0:T(128)}) custom-call(f32[2,4096]{1,0:T(2,128)} %rep_hbm.1, s32[2,2]{1,0:T(2,128)} %thresh_hbm.1, s32[2,2]{1,0:T(2,128)} %window_hbm.1, s32[2,2,128,4096]{3,2,1,0:T(8,128)} %x_hbm.1, f32[2,32,128]{2,1,0:T(8,128)} %constant.8.clone.tw_hbm, bf16[768,256]{1,0:T(8,128)(2,1)} %constant.9.clone.wf_hbm, ...), custom_call_target="tpu_custom_call" | custom-call | flops 20000000000 | bytes 33554432 | tf_op jit(solution)/shard_map/pallas_call | solution.py:516
  198.9 2.0 copy.12

commit v3 on v2

--- a/solution.py
+++ b/solution.py
@@ -26,7 +26,7 @@
 
 
 MESH = pl.DeviceIdType.MESH
-ROWS = 16
+ROWS = 8
 AHEAD = 3
 
 
@@ -170,24 +170,26 @@
     h = n // 2
     half = z // h
 
-    def peer(p):
-        i = lax.rem(me + p, peers)
-        return {"pulse": i // (nx * ns), "chan": lax.rem(i // ns, nx), "sub": lax.rem(i, ns)}
+    def others(act):
+        def along(o, carry):
+            for ox in range(nx):
+                for os in range(ns):
+                    act({"pulse": lax.rem(z + o, n), "chan": lax.rem(x + ox, nx), "sub": lax.rem(s + os, ns)})
+            return carry
+        lax.fori_loop(1, n, along, 0, unroll=n <= 4)
+        for ox in range(nx):
+            for os in range(ns):
+                if ox or os:
+                    act({"pulse": z, "chan": lax.rem(x + ox, nx), "sub": lax.rem(s + os, ns)})
 
     barrier = pltpu.get_barrier_semaphore()
 
-    def greet(p, carry):
-        pl.semaphore_signal(barrier, 1, device_id=peer(p), device_id_type=MESH)
-        return carry
+    others(lambda who: pl.semaphore_signal(barrier, 1, device_id=who, device_id_type=MESH))
 
     def load(b):
         c = b // blocks
         r = pl.ds(pl.multiple_of(lax.rem(b, blocks) * rows, rows), rows)
         return pltpu.make_async_copy(x_hbm.at[:, c, r, :], xs.at[:, c, r, :], in_sem.at[b])
-
-    def start_load(b, carry):
-        load(b).start()
-        return carry
 
     tables = [pltpu.make_async_copy(a, b, tab_sem.at[i])
               for i, (a, b) in enumerate(((rep_hbm, rep), (tw_hbm, tw), (wf_hbm, wf), (wi_hbm, wi), (t_hbm, table),
@@ -196,10 +198,8 @@
     load(0).start()
     for copy in tables[1:4]:
         copy.start()
-    lax.fori_loop(1, peers, greet, 0)
-    lax.fori_loop(1, channels * blocks, start_load, 0)
-    for copy in tables[4:]:
-        copy.start()
+    for b in range(1, min(2, channels * blocks)):
+        load(b).start()
     cols = tw.shape[1]
     nat[...] = jnp.zeros_like(nat)
     tables[0].wait()
@@ -265,10 +265,16 @@
         r0 = lax.rem(b, blocks) * rows
         load(b).wait()
 
+        @pl.when(b + 2 < channels * blocks)
+        def _():
+            load(b + 2).start()
+
         @pl.when(b == 0)
         def _():
             tables[2].wait()
             tables[3].wait()
+            for copy in tables[4:]:
+                copy.start()
 
         for u in range(rows // SUB):
             range_rows(xs, c, pl.multiple_of(r0 + u * SUB, SUB), tw8, rep8, wf, wi, comp)
@@ -459,9 +465,25 @@
     if chunks >= 4:
         arrive(chunks - 1)
         dop(last, order(jnp.int32(chunks - 1)))
-        each(lambda k: cfar(last, order(k)), chunks - 3, chunks)
+        for k in range(chunks - 3, chunks):
+            cfar(last, (k % 2) * (chunks - 1) + (1 - 2 * (k % 2)) * (k // 2))
 
     gather[me] = jnp.sum(acc[...], axis=0, keepdims=True)
+    for c in range(channels):
+        @pl.when(z > 0)
+        def _():
+            halo_copy(c, 0, z - 1).wait_send()
+
+        @pl.when(z < n - 1)
+        def _():
+            halo_copy(c, 1, z + 1).wait_send()
+
+    def tell(who):
+        pltpu.make_async_remote_copy(
+            gather.at[me], gather.at[me], sum_sem.at[0], sum_sem.at[1],
+            device_id=who, device_id_type=MESH).start()
+
+    others(tell)
     for c in range(last):
         for o in range(1, n):
             row_all(c, lax.rem(z + o, n), z).wait_send()
@@ -471,27 +493,39 @@
             chunk_copy(lax.rem(z + o, n), z, g).wait_send()
 
     each(sent, 0, chunks)
-    for c in range(channels):
-        @pl.when(z > 0)
-        def _():
-            halo_copy(c, 0, z - 1).wait_send()
-
-        @pl.when(z < n - 1)
-        def _():
-            halo_copy(c, 1, z + 1).wait_send()
-
-    def tell(p):
-        pltpu.make_async_remote_copy(
-            gather.at[me], gather.at[me], sum_sem.at[0], sum_sem.at[1],
-            device_id=peer(p), device_id_type=MESH).start()
-
-    each(tell, 1, peers)
     every = pltpu.make_async_remote_copy(
         gather.at[pl.ds(0, peers - 1)], gather.at[pl.ds(0, peers - 1)], sum_sem.at[0], sum_sem.at[1],
-        device_id=peer(1), device_id_type=MESH)
-    every.wait()
+        device_id={"pulse": lax.rem(z + 1, n)}, device_id_type=MESH)
+    every.wait_recv()
     total = jnp.sum(gather[...], axis=0)
-    count[0] = jnp.sum(total) * (1024.0 / (pulses * gates))
+    total = jnp.sum(total, axis=1, keepdims=True) * (1024.0 / (pulses * gates))
+    count[...] = jnp.broadcast_to(total, count.shape)
+    every.wait_send()
+
+
+def deliver_kernel(ratio, count, ratio_out, count_out, one, sem):
+    channels, pulses, _ = ratio.shape
+    step = pulses // 8
+    one[0] = count[0, 0]
+    copies = [pltpu.make_async_copy(one, count_out, sem.at[0])]
+    for i in range(8 * channels):
+        c, r = i // 8, pl.ds(i % 8 * step, step)
+        copies.append(pltpu.make_async_copy(ratio.at[c, r], ratio_out.at[c, r], sem.at[i + 1]))
+    for copy in copies:
+        copy.start()
+    for copy in copies:
+        copy.wait()
+
+
+def deliver(ratio, count):
+    return pl.pallas_call(
+        deliver_kernel,
+        in_specs=[pl.BlockSpec(memory_space=pltpu.VMEM)] * 2,
+        out_specs=[pl.BlockSpec(memory_space=pltpu.HBM)] * 2,
+        out_shape=[jax.ShapeDtypeStruct(ratio.shape, jnp.float32), jax.ShapeDtypeStruct((1,), jnp.float32)],
+        scratch_shapes=[pltpu.SMEM((1,), jnp.float32), pltpu.SemaphoreType.DMA((8 * ratio.shape[0] + 1,))],
+        compiler_params=pltpu.CompilerParams(vmem_limit_bytes=1 << 20),
+    )(*(pltpu.with_memory_space_constraint(a, pltpu.VMEM) for a in (ratio, count)))
 
 
 def local(samples, replica, window, thresh):
@@ -511,13 +545,13 @@
     table = doppler_table(pulses)
     peers = n * nx * ns
     f32, bf16 = jnp.float32, jnp.bfloat16
-    smem, vmem, hbm = (pl.BlockSpec(memory_space=m) for m in (pltpu.SMEM, pltpu.VMEM, pltpu.HBM))
+    vmem, hbm = (pl.BlockSpec(memory_space=m) for m in (pltpu.VMEM, pltpu.HBM))
     dma = pltpu.SemaphoreType.DMA
-    return pl.pallas_call(
+    return deliver(*pl.pallas_call(
         functools.partial(kernel, (n, nx, ns, rows)),
         in_specs=[hbm] * 8,
-        out_specs=[vmem, smem],
-        out_shape=[pltpu.VMEM((channels, pulses, own), f32), jax.ShapeDtypeStruct((1,), f32)],
+        out_specs=[vmem, vmem],
+        out_shape=[pltpu.VMEM((channels, pulses, own), f32), pltpu.VMEM((1, LANES), f32)],
         scratch_shapes=[
             pltpu.VMEM(replica.shape, f32),
             pltpu.SMEM(thresh.shape, jnp.int32),
@@ -555,7 +589,7 @@
             collective_id=0, has_side_effects=True, vmem_limit_bytes=48 << 20),
         cost_estimate=pl.CostEstimate(flops=int(2e10), bytes_accessed=32 << 20, transcendentals=0),
     )(*(pltpu.with_memory_space_constraint(jnp.asarray(a), pltpu.HBM)
-        for a in (replica, thresh, window, samples, tw, wf, wi, table)))
+        for a in (replica, thresh, window, samples, tw, wf, wi, table))))
 
 
 def solution(mesh):

time: 203 us -> 200 us (0.985)
    pallas_call x0 -> x1, Pallas kernels: none -> 2.18 us  [deliver(): pl.pallas_call(deliver_kernel, in_specs=[pl.BlockSpec(memory_space=pltpu....]
where the time goes in v3:
time: 200 us
  Pallas kernels  200 us (100%)
    pallas_call x1, Pallas kernels, local(): pl.pallas_call(functools.partial(kernel, (n, nx, ns, rows)), in_specs=[hb...  197 us

profile of v3, /device:TPU:0, one launch (start us, length us, event | category | flops | bytes accessed | tf_op | source)
XLA Modules:
  0.0 200.2 jit_solution(3303974090794376855)
XLA Ops:
  0.6 197.4 %shard_map.95 = (f32[2,512,1024]{2,1,0:T(8,128)S(1)}, f32[1,128]{1,0:T(1,128)S(1)}) custom-call(f32[2,4096]{1,0:T(2,128)} %rep_hbm.1, s32[2,2]{1,0:T(2,128)} %thresh_hbm.1, s32[2,2]{1,0:T(2,128)} %window_hbm.1, s32[2,2,128,4096]{3,2,1,0:T(8,128)} %x_hbm.1, f32[2,32,128]{2,1,0:T(8,128)} %constant.8.clone.tw_hbm, bf16[768,256]{1,0:T(8,128)(2,1)} %constant.9.clone.wf_hbm, ...), custom_call_target="tpu_custom_call" | custom-call | flops 20000000000 | bytes 33554432 | tf_op jit(solution)/shard_map/pallas_call | solution.py:550
  198.0 2.2 %shard_map.96 = (f32[2,512,1024]{2,1,0:T(8,128)}, f32[1]{0:T(128)}) custom-call(f32[2,512,1024]{2,1,0:T(8,128)S(1)} %get-tuple-element.4.ratio, f32[1,128]{1,0:T(1,128)S(1)} %get-tuple-element.5.count), custom_call_target="tpu_custom_call" | custom-call | tf_op jit(solution)/shard_map/pallas_call | solution.py:521

commit v4 on v3

--- a/solution.py
+++ b/solution.py
@@ -48,7 +48,7 @@
         c, s = np.cos(ang) / math.sqrt(pulses), -np.sin(ang) / math.sqrt(pulses)
         full = np.block([[c, -s], [s, c]])
         hi, lo = halves(full)
-        out.append(np.concatenate([hi, hi, lo], axis=1))
+        out.append(np.concatenate([hi, lo], axis=1))
     return np.stack(out)
 
 
@@ -124,7 +124,12 @@
     ys = [(sr + ur, si + ui), (dr + vi, di - vr), (sr - ur, si - ui), (dr - vi, di + vr)]
     for res in range(RADIX):
         y = jnp.concatenate(ys[res], axis=0)
-        out = jnp.dot(table[res], split(y, 0), preferred_element_type=jnp.float32)
+        near = y.astype(jnp.bfloat16)
+        both = jnp.concatenate([near, (y - near.astype(jnp.float32)).astype(jnp.bfloat16)], axis=1)
+        width = y.shape[0]
+        main = jnp.dot(table[res, :, :width], both, preferred_element_type=jnp.float32)
+        rest = jnp.dot(table[res, :, width:], near, preferred_element_type=jnp.float32)
+        out = main[:, :LANES] + main[:, LANES:] + rest
         re, im = out[:quarter], out[quarter:]
         p = re * re + im * im
         hi = p.astype(jnp.bfloat16)
@@ -170,21 +175,27 @@
     h = n // 2
     half = z // h
 
-    def others(act):
-        def along(o, carry):
-            for ox in range(nx):
-                for os in range(ns):
-                    act({"pulse": lax.rem(z + o, n), "chan": lax.rem(x + ox, nx), "sub": lax.rem(s + os, ns)})
+    def each(body, lo, hi):
+        def run(i, carry):
+            body(i)
             return carry
-        lax.fori_loop(1, n, along, 0, unroll=n <= 4)
+        lax.fori_loop(lo, hi, run, 0, unroll=hi - lo < 4)
+
+    def beside(act):
         for ox in range(nx):
             for os in range(ns):
                 if ox or os:
                     act({"pulse": z, "chan": lax.rem(x + ox, nx), "sub": lax.rem(s + os, ns)})
 
+    def others(act):
+        def along(o):
+            for ox in range(nx):
+                for os in range(ns):
+                    act({"pulse": lax.rem(z + n - o, n), "chan": lax.rem(x + ox, nx), "sub": lax.rem(s + os, ns)})
+        each(along, 1, n)
+        beside(act)
+
     barrier = pltpu.get_barrier_semaphore()
-
-    others(lambda who: pl.semaphore_signal(barrier, 1, device_id=who, device_id_type=MESH))
 
     def load(b):
         c = b // blocks
@@ -198,6 +209,11 @@
     load(0).start()
     for copy in tables[1:4]:
         copy.start()
+    def greet(who):
+        pl.semaphore_signal(barrier, 1, device_id=who, device_id_type=MESH)
+
+    each(lambda o: greet({"pulse": lax.rem(z + o, n)}), 1, n)
+    beside(greet)
     for b in range(1, min(2, channels * blocks)):
         load(b).start()
     cols = tw.shape[1]
@@ -210,13 +226,18 @@
     row = lax.broadcasted_iota(jnp.int32, (LANES, LANES), 0)
     lane = lax.broadcasted_iota(jnp.int32, (LANES, LANES), 1)
     per = LANES // cols
+    pick = [jnp.where(jnp.logical_and(row >= ri * cols, lane == per * (row - ri * cols)), 1.0, 0.0) for ri in range(2)]
+    pick = jnp.concatenate(pick, axis=1).astype(jnp.bfloat16)
+    terms = []
+    for _ in range(3):
+        terms.append(turned.astype(jnp.bfloat16))
+        turned = turned - terms[-1].astype(jnp.float32)
+    placed = jnp.dot(jnp.concatenate(terms, axis=1), jnp.concatenate([pick] * 3, axis=0),
+                     preferred_element_type=jnp.float32) * (INPUT_SCALE / gates)
     for ri in range(2):
-        filt = jnp.zeros((cols, LANES), jnp.float32)
-        for k in range(per):
-            pick = jnp.where(jnp.logical_and(row >= ri * cols, lane == per * (row - ri * cols) + k), 1.0, 0.0)
-            filt = filt + jnp.dot(turned[k * cols:(k + 1) * cols], pick, precision=lax.Precision.HIGHEST,
-                                  preferred_element_type=jnp.float32)
-        filt = filt * (INPUT_SCALE / gates)
+        filt = placed[:cols, ri * LANES:(ri + 1) * LANES]
+        for k in range(1, per):
+            filt = filt + pltpu.roll(placed[k * cols:(k + 1) * cols, ri * LANES:(ri + 1) * LANES], k, 1)
         for k in range(cols):
             rep8[ri, k * SUB:(k + 1) * SUB, :] = jnp.broadcast_to(filt[k:k + 1, :], (SUB, LANES))
     tables[1].wait()
@@ -279,13 +300,13 @@
         for u in range(rows // SUB):
             range_rows(xs, c, pl.multiple_of(r0 + u * SUB, SUB), tw8, rep8, wf, wi, comp)
 
-        @pl.when(b == 1)
-        def _():
-            pl.semaphore_wait(barrier, peers - 1)
-
-        @pl.when(jnp.logical_and(b >= 1, b <= last * blocks))
-        def _():
-            pc, pb = (b - 1) // blocks, lax.rem(b - 1, blocks)
+        @pl.when(b == 0)
+        def _():
+            pl.semaphore_wait(barrier, n - 1 + nx * ns - 1)
+
+        @pl.when(b < last * blocks)
+        def _():
+            pc, pb = c, lax.rem(b, blocks)
 
             @pl.when(outer)
             def _():
@@ -299,12 +320,6 @@
 
     lax.fori_loop(0, channels * blocks, step, 0)
 
-    def each(body, lo, hi):
-        def run(i, carry):
-            body(i)
-            return carry
-        lax.fori_loop(lo, hi, run, 0)
-
     def order(k):
         odd = lax.rem(k, 2)
         return odd * (chunks - 1) + (1 - 2 * odd) * (k // 2)
@@ -325,7 +340,7 @@
             chunk_copy(near(q), z, order(k)).start()
 
     def far(q):
-        return (1 - half) * (n - 1 - q) + half * q
+        return (2 - half) * h - 1 - q
 
     def last_cross(k):
         end = k // (chunks - 1) if chunks > 1 else 1

time: 200 us -> 199 us (level)
  Pallas kernels: 200 us -> 198 us
where the time goes in v4:
time: 199 us
  Pallas kernels  198 us (99%)
    pallas_call x1, Pallas kernels, local(): pl.pallas_call(functools.partial(kernel, (n, nx, ns, rows)), in_specs=[hb...  196 us

profile of v4, /device:TPU:0, one launch (start us, length us, event | category | flops | bytes accessed | tf_op | source)
XLA Modules:
  0.0 199.0 jit_solution(2740580878568391237)
XLA Ops:
  0.6 196.2 %shard_map.95 = (f32[2,512,1024]{2,1,0:T(8,128)S(1)}, f32[1,128]{1,0:T(1,128)S(1)}) custom-call(f32[2,4096]{1,0:T(2,128)} %rep_hbm.1, s32[2,2]{1,0:T(2,128)} %thresh_hbm.1, s32[2,2]{1,0:T(2,128)} %window_hbm.1, s32[2,2,128,4096]{3,2,1,0:T(8,128)} %x_hbm.1, f32[2,32,128]{2,1,0:T(8,128)} %constant.8.clone.tw_hbm, bf16[768,256]{1,0:T(8,128)(2,1)} %constant.9.clone.wf_hbm, ...), custom_call_target="tpu_custom_call" | custom-call | flops 20000000000 | bytes 33554432 | tf_op jit(solution)/shard_map/pallas_call | solution.py:565
  196.8 2.2 %shard_map.96 = (f32[2,512,1024]{2,1,0:T(8,128)}, f32[1]{0:T(128)}) custom-call(f32[2,512,1024]{2,1,0:T(8,128)S(1)} %get-tuple-element.4.ratio, f32[1,128]{1,0:T(1,128)S(1)} %get-tuple-element.5.count), custom_call_target="tpu_custom_call" | custom-call | tf_op jit(solution)/shard_map/pallas_call | solution.py:536

commit v5 on v4

--- a/solution.py
+++ b/solution.py
@@ -340,7 +340,7 @@
             chunk_copy(near(q), z, order(k)).start()
 
     def far(q):
-        return (2 - half) * h - 1 - q
+        return (1 - half) * (n - 1 - q) + half * q
 
     def last_cross(k):
         end = k // (chunks - 1) if chunks > 1 else 1
@@ -521,13 +521,15 @@
 def deliver_kernel(ratio, count, ratio_out, count_out, one, sem):
     channels, pulses, _ = ratio.shape
     step = pulses // 8
-    one[0] = count[0, 0]
-    copies = [pltpu.make_async_copy(one, count_out, sem.at[0])]
+    copies = []
     for i in range(8 * channels):
         c, r = i // 8, pl.ds(i % 8 * step, step)
         copies.append(pltpu.make_async_copy(ratio.at[c, r], ratio_out.at[c, r], sem.at[i + 1]))
     for copy in copies:
         copy.start()
+    one[0] = count[0, 0]
+    copies.append(pltpu.make_async_copy(one, count_out, sem.at[0]))
+    copies[-1].start()
     for copy in copies:
         copy.wait()
 

time: 199 us -> 199 us (level)
  no operation moved by 1% of the time
where the time goes in v5:
time: 199 us
  Pallas kernels  198 us (99%)
    pallas_call x1, Pallas kernels, local(): pl.pallas_call(functools.partial(kernel, (n, nx, ns, rows)), in_specs=[hb...  196 us

profile of v5, /device:TPU:0, one launch (start us, length us, event | category | flops | bytes accessed | tf_op | source)
XLA Modules:
  0.0 198.9 jit_solution(14665223897631100966)
XLA Ops:
  0.6 196.1 %shard_map.95 = (f32[2,512,1024]{2,1,0:T(8,128)S(1)}, f32[1,128]{1,0:T(1,128)S(1)}) custom-call(f32[2,4096]{1,0:T(2,128)} %rep_hbm.1, s32[2,2]{1,0:T(2,128)} %thresh_hbm.1, s32[2,2]{1,0:T(2,128)} %window_hbm.1, s32[2,2,128,4096]{3,2,1,0:T(8,128)} %x_hbm.1, f32[2,32,128]{2,1,0:T(8,128)} %constant.8.clone.tw_hbm, bf16[768,256]{1,0:T(8,128)(2,1)} %constant.9.clone.wf_hbm, ...), custom_call_target="tpu_custom_call" | custom-call | flops 20000000000 | bytes 33554432 | tf_op jit(solution)/shard_map/pallas_call | solution.py:567
  196.7 2.2 %shard_map.96 = (f32[2,512,1024]{2,1,0:T(8,128)}, f32[1]{0:T(128)}) custom-call(f32[2,512,1024]{2,1,0:T(8,128)S(1)} %get-tuple-element.4.ratio, f32[1,128]{1,0:T(1,128)S(1)} %get-tuple-element.5.count), custom_call_target="tpu_custom_call" | custom-call | tf_op jit(solution)/shard_map/pallas_call | solution.py:538

commit v6 on v5

--- a/solution.py
+++ b/solution.py
@@ -138,7 +138,7 @@
         lo_ref[c, g + 1, res] = (p - hi.astype(jnp.float32)).astype(jnp.bfloat16)
 
 
-def cfar_chunk(c, g, first_gate, gates, thresh, window, pw, hi_ref, lo_ref, band, stage, out, acc):
+def cfar_chunk(c, g, first_gate, gates, thresh, window, pw, hi_ref, lo_ref, band, acc):
     quarter = pw.shape[3]
     total = RADIX * quarter
     parts = [ref[c, g + k].reshape(total, LANES) for ref in (hi_ref, lo_ref) for k in range(3)]
@@ -151,11 +151,16 @@
     cells = cells.astype(jnp.float32)[:1]
     inv = thresh[c, 1].astype(jnp.float32) / thresh[c, 0].astype(jnp.float32)
     ratio = pw[c, g].reshape(total, LANES) * cells / (noise + EPSILON)
-    for res in range(RADIX):
-        stage[pl.ds(res, quarter, stride=RADIX), :] = ratio[res * quarter:(res + 1) * quarter]
-    out[c, :, pl.ds(pl.multiple_of(g * LANES, LANES), LANES)] = stage[...]
+    pw[c, g] = ratio.reshape(RADIX, quarter, LANES)
     soft = jnp.clip(ratio * inv - 1.0, 0.0, 1.0)
     acc[...] += jnp.sum(soft.reshape(total // SUB, SUB, LANES), axis=0)
+
+
+def place_chunk(c, g, pw, stage, out):
+    quarter = pw.shape[3]
+    for res in range(RADIX):
+        stage[pl.ds(res, quarter, stride=RADIX), :] = pw[c, g, res]
+    out[c, :, pl.ds(pl.multiple_of(g * LANES, LANES), LANES)] = stage[...]
 
 
 def kernel(sizes, rep_hbm, thresh_hbm, window_hbm, x_hbm, tw_hbm, wf_hbm, wi_hbm, t_hbm, out, count,
@@ -378,8 +383,12 @@
     def dop(c, g):
         doppler_chunk(recv, c, g, table, pw, hi_ref, lo_ref)
 
+    def rate(c, g):
+        cfar_chunk(c, g, z * own, gates, thresh, window, pw, hi_ref, lo_ref, band, acc)
+
     def cfar(c, g):
-        cfar_chunk(c, g, z * own, gates, thresh, window, pw, hi_ref, lo_ref, band, stage, out, acc)
+        rate(c, g)
+        place_chunk(c, g, pw, stage, out)
 
     def pack_left(c):
         pack[c, 0] = jnp.concatenate([pw[c, 0, res][:, :MARGIN] for res in range(RADIX)], axis=1)
@@ -481,7 +490,7 @@
         arrive(chunks - 1)
         dop(last, order(jnp.int32(chunks - 1)))
         for k in range(chunks - 3, chunks):
-            cfar(last, (k % 2) * (chunks - 1) + (1 - 2 * (k % 2)) * (k // 2))
+            rate(last, (k % 2) * (chunks - 1) + (1 - 2 * (k % 2)) * (k // 2))
 
     gather[me] = jnp.sum(acc[...], axis=0, keepdims=True)
     for c in range(channels):
@@ -499,6 +508,8 @@
             device_id=who, device_id_type=MESH).start()
 
     others(tell)
+    if chunks >= 4:
+        each(lambda k: place_chunk(last, order(k), pw, stage, out), chunks - 3, chunks)
     for c in range(last):
         for o in range(1, n):
             row_all(c, lax.rem(z + o, n), z).wait_send()

time: 199 us -> 199 us (level)
  no operation moved by 1% of the time
where the time goes in v6:
time: 199 us
  Pallas kernels  198 us (99%)
    pallas_call x1, Pallas kernels, local(): pl.pallas_call(functools.partial(kernel, (n, nx, ns, rows)), in_specs=[hb...  196 us

profile of v6, /device:TPU:0, one launch (start us, length us, event | category | flops | bytes accessed | tf_op | source)
XLA Modules:
  0.0 198.8 jit_solution(12074505091722877803)
XLA Ops:
  0.6 196.0 %shard_map.95 = (f32[2,512,1024]{2,1,0:T(8,128)S(1)}, f32[1,128]{1,0:T(1,128)S(1)}) custom-call(f32[2,4096]{1,0:T(2,128)} %rep_hbm.1, s32[2,2]{1,0:T(2,128)} %thresh_hbm.1, s32[2,2]{1,0:T(2,128)} %window_hbm.1, s32[2,2,128,4096]{3,2,1,0:T(8,128)} %x_hbm.1, f32[2,32,128]{2,1,0:T(8,128)} %constant.8.clone.tw_hbm, bf16[768,256]{1,0:T(8,128)(2,1)} %constant.9.clone.wf_hbm, ...), custom_call_target="tpu_custom_call" | custom-call | flops 20000000000 | bytes 33554432 | tf_op jit(solution)/shard_map/pallas_call | solution.py:578
  196.7 2.2 %shard_map.96 = (f32[2,512,1024]{2,1,0:T(8,128)}, f32[1]{0:T(128)}) custom-call(f32[2,512,1024]{2,1,0:T(8,128)S(1)} %get-tuple-element.4.ratio, f32[1,128]{1,0:T(1,128)S(1)} %get-tuple-element.5.count), custom_call_target="tpu_custom_call" | custom-call | tf_op jit(solution)/shard_map/pallas_call | solution.py:549
